TPU v7x, 32 devices: a 4x2x2 block of a 4x4x8 slice. The times are simulated.
32 devices in a mesh: dp: 4 (over y, z), tp: 8 (over x, core).
Axes of the slice: x: 4, y: 2, z: 2, core: 2. Of those that a mesh axis runs over, the one named last changes fastest.
The devices are a block of a 4x4x8 slice.
Arguments:
- hidden: bfloat16 [64, 64, 2048], P('dp'), parts along dimension 0
- tree_mask: int32 [64, 64, 64], P('dp'), parts along dimension 0
- depth: int32 [64, 64], P('dp'), parts along dimension 0
- ctx_len: int32 [64], P('dp'), parts along dimension 0
- block_table: int32 [64, 24], P('dp'), parts along dimension 0
- score_id: int32 [64, 64], P('dp'), parts along dimension 0
- k_cache: bfloat16 [1536, 16, 8, 64], P('dp', None, 'tp'), parts along dimension 0
- v_cache: bfloat16 [1536, 16, 8, 64], P('dp', None, 'tp'), parts along dimension 0
- attn_norm: bfloat16 [2048], replicated
- w_q: bfloat16 [2048, 2048], P(None, 'tp')
- w_k: bfloat16 [2048, 512], P(None, 'tp')
- w_v: bfloat16 [2048, 512], P(None, 'tp')
- w_o: bfloat16 [2048, 2048], P('tp')
- mlp_norm: bfloat16 [2048], replicated
- w_gate: bfloat16 [2048, 8192], P(None, 'tp')
- w_up: bfloat16 [2048, 8192], P(None, 'tp')
- w_down: bfloat16 [8192, 2048], P('tp')
- final_norm: bfloat16 [2048], replicated
- w_lm: bfloat16 [2048, 128256], P(None, 'tp')
Outputs:
- output 1: float32 [64, 64], P('dp'), parts along dimension 0
- output 2: float32 [64, 64], P('dp'), parts along dimension 0
- output 3: bfloat16 [1536, 16, 8, 64], P('dp', None, 'tp'), parts along dimension 0
- output 4: bfloat16 [1536, 16, 8, 64], P('dp', None, 'tp'), parts along dimension 0
There are 4 independent parts. A program takes and returns all parts, laid end to end along the dimension named above; an argument that names none is the same for every part.
All inputs are finite; a program needn't handle non-finite values.
Results may differ from a plain program's by a relative error of at most 0.00344325.
Values are sent between devices in bfloat16 or wider.
A program may use at most 768 MiB of HBM per device.

v0:
```python
import jax
import jax.numpy as jnp
from jax import lax
from jax.sharding import PartitionSpec as P

RMS_EPS = 1e-5
ROPE_THETA = 500000


def rms_norm(values, gain):
    widened = values.astype(jnp.float32)
    scale = lax.rsqrt(jnp.mean(widened * widened, axis=-1, keepdims=True) + RMS_EPS)
    return (widened * scale * gain.astype(jnp.float32)).astype(jnp.bfloat16)


def rotate(values, positions):
    head_dim = values.shape[-1]
    half = head_dim // 2
    inv_freq = 1.0 / (ROPE_THETA ** (jnp.arange(half, dtype=jnp.float32) * (2.0 / head_dim)))
    angles = positions.astype(jnp.float32)[..., None] * inv_freq
    cosine = jnp.cos(angles)[..., None, :]
    sine = jnp.sin(angles)[..., None, :]
    first = values[..., :half]
    second = values[..., half:]
    return jnp.concatenate([first * cosine - second * sine, second * cosine + first * sine], axis=-1)


def tree_attention(query, key_new, val_new, key_old, val_old, tree_mask, ctx_len):
    scale = query.shape[-1] ** -0.5
    span = key_old.shape[1]
    score_old = jnp.einsum("btkgh,bskh->btkgs", query, key_old, preferred_element_type=jnp.float32) * scale
    seen_old = jnp.arange(span)[None, :] < ctx_len[:, None]
    score_old = jnp.where(seen_old[:, None, None, None, :], score_old, -jnp.inf)
    score_new = jnp.einsum("btkgh,bjkh->btkgj", query, key_new, preferred_element_type=jnp.float32) * scale
    score_new = jnp.where((tree_mask > 0)[:, :, None, None, :], score_new, -jnp.inf)
    top = jnp.maximum(jnp.max(score_old, axis=-1), jnp.max(score_new, axis=-1))[..., None]
    prob_old = jnp.exp(score_old - top)
    prob_new = jnp.exp(score_new - top)
    total = jnp.sum(prob_old, axis=-1) + jnp.sum(prob_new, axis=-1)
    mixed = jnp.einsum("btkgs,bskh->btkgh", prob_old.astype(jnp.bfloat16), val_old, preferred_element_type=jnp.float32)
    mixed = mixed + jnp.einsum("btkgj,bjkh->btkgh", prob_new.astype(jnp.bfloat16), val_new, preferred_element_type=jnp.float32)
    return (mixed / total[..., None]).astype(jnp.bfloat16)


def write_cache(cache, table, ctx_len, new_rows):
    page_size = cache.shape[1]
    slots = ctx_len[:, None] + jnp.arange(new_rows.shape[1])[None, :]
    slot_blocks = jnp.take_along_axis(table, slots // page_size, axis=1)
    return cache.at[slot_blocks, slots % page_size].set(new_rows)


def layer_and_logits(hidden, tree_mask, depth, ctx_len, block_table, k_cache, v_cache, attn_norm, w_q, w_k, w_v, w_o, mlp_norm, w_gate, w_up, w_down, final_norm, w_lm):
    requests = hidden.shape[0]
    nodes = hidden.shape[1]
    page_size = k_cache.shape[1]
    kv_local = k_cache.shape[2]
    head_dim = k_cache.shape[3]
    span = block_table.shape[1] * page_size
    heads_local = w_q.shape[1] // head_dim
    normed = rms_norm(hidden, attn_norm)
    positions = ctx_len[:, None] + depth
    query = jnp.dot(normed, w_q, preferred_element_type=jnp.float32).reshape(requests, nodes, heads_local, head_dim)
    query = rotate(query, positions).astype(jnp.bfloat16).reshape(requests, nodes, kv_local, heads_local // kv_local, head_dim)
    key_new = jnp.dot(normed, w_k, preferred_element_type=jnp.float32).reshape(requests, nodes, kv_local, head_dim)
    key_new = rotate(key_new, positions).astype(jnp.bfloat16)
    val_new = jnp.dot(normed, w_v, preferred_element_type=jnp.float32).astype(jnp.bfloat16).reshape(requests, nodes, kv_local, head_dim)
    key_old = k_cache[block_table].reshape(requests, span, kv_local, head_dim)
    val_old = v_cache[block_table].reshape(requests, span, kv_local, head_dim)
    attended = tree_attention(query, key_new, val_new, key_old, val_old, tree_mask, ctx_len).reshape(requests, nodes, heads_local * head_dim)
    attn_sum = lax.psum(jnp.dot(attended, w_o, preferred_element_type=jnp.float32).astype(jnp.bfloat16), "tp")
    residual = (hidden.astype(jnp.float32) + attn_sum.astype(jnp.float32)).astype(jnp.bfloat16)
    normed_mlp = rms_norm(residual, mlp_norm)
    gate = jnp.dot(normed_mlp, w_gate, preferred_element_type=jnp.float32)
    upper = jnp.dot(normed_mlp, w_up, preferred_element_type=jnp.float32)
    product = (jax.nn.silu(gate) * upper).astype(jnp.bfloat16)
    mlp_sum = lax.psum(jnp.dot(product, w_down, preferred_element_type=jnp.float32).astype(jnp.bfloat16), "tp")
    layer_out = (residual.astype(jnp.float32) + mlp_sum.astype(jnp.float32)).astype(jnp.bfloat16)
    logits = jnp.dot(rms_norm(layer_out, final_norm), w_lm, preferred_element_type=jnp.float32)
    return logits, key_new, val_new


def solution(mesh):
    def group_step(hidden, tree_mask, depth, ctx_len, block_table, score_id, k_cache, v_cache, attn_norm, w_q, w_k, w_v, w_o, mlp_norm, w_gate, w_up, w_down, final_norm, w_lm):
        logits, key_new, val_new = layer_and_logits(hidden, tree_mask, depth, ctx_len, block_table, k_cache, v_cache, attn_norm, w_q, w_k, w_v, w_o, mlp_norm, w_gate, w_up, w_down, final_norm, w_lm)
        vocab_local = logits.shape[-1]
        global_top = lax.pmax(jnp.max(logits, axis=-1), "tp")
        part_sum = jnp.sum(jnp.exp(logits - global_top[..., None]), axis=-1)
        local_id = score_id - lax.axis_index("tp") * vocab_local
        inside = (local_id >= 0) & (local_id < vocab_local)
        picked = jnp.take_along_axis(logits, jnp.clip(local_id, 0, vocab_local - 1)[..., None], axis=-1)[..., 0]
        summed = lax.psum(jnp.stack([part_sum, jnp.where(inside, picked, 0.0)]), "tp")
        log_norm = global_top + jnp.log(summed[0])
        log_prob = summed[1] - log_norm
        return log_norm, log_prob, write_cache(k_cache, block_table, ctx_len, key_new), write_cache(v_cache, block_table, ctx_len, val_new)

    request_spec = P("dp", None, None)
    node_spec = P("dp", None)
    cache_spec = P("dp", None, "tp", None)
    shared_spec = P(None)
    column_spec = P(None, "tp")
    row_spec = P("tp", None)
    in_specs = (request_spec, request_spec, node_spec, P("dp"), node_spec, node_spec, cache_spec, cache_spec, shared_spec, column_spec, column_spec, column_spec, row_spec, shared_spec, column_spec, column_spec, row_spec, shared_spec, column_spec)
    out_specs = (node_spec, node_spec, cache_spec, cache_spec)
    return jax.shard_map(group_step, mesh=mesh, in_specs=in_specs, out_specs=out_specs, check_vma=False)
```

profile of v0, /device:TPU:80, one launch (start us, length us, event | category | flops | bytes accessed | tf_op | source)
XLA Modules:
  0.0 402.2 jit_solution(4100383376545345638)
XLA Ops:
  7.2 0.0 copy-start
  7.2 0.1 all-reduce.3.cloned.1.call-start
  7.3 1.4 iota_compare_fusion
  8.7 0.8 bitcast_or_fusion
  9.5 0.7 convert_element_type.84
  10.2 0.7 compare_select_fusion.4
  10.9 0.1 reshape.320
  11.0 3.1 fusion.5
  14.1 0.1 reshape.387
  14.2 7.1 %gather_fusion.3 = s32[1024]{0:T(1024)S(1)} fusion(s32[16,24]{1,0:T(8,128)S(1)} %copy-done.2, s32[1024]{0:T(1024)S(1)} %reshape.387), kind=kCustom, calls=%fused_computation.clone | custom fusion | bytes 16384 | tf_op jit(solution)/shard_map/jit(take_along_axis)/gather | solution.py:48
  21.2 0.1 reshape.390
  21.3 0.1 broadcast_compare_fusion
  21.4 0.3 copy.35
  21.7 4.4 %fusion.59 = bf16[16,64,64]{2,1,0:T(8,128)(2,1)} fusion(bf16[16,64,2048]{2,1,0:T(8,128)(2,1)} %param.21, f32[2048]{0:T(1024)S(1)} %convert_element_type.84, f32[16,64]{1,0:T(8,128)S(1)} %add_rsqrt_fusion.2, bf16[2048,64]{0,1:T(8,128)(2,1)S(1)} %copy-done.21), kind=kOutput, calls=%fused_computation.64 | convolution fusion | flops 276889600 | bytes 4599808 | tf_op jit(solution)/shard_map/dot_general | solution.py:66
  26.1 2.2 fusion.56
  28.3 0.7 fusion.83
  29.0 2.9 multiply_cosine_fusion
  31.9 1.2 fusion.72
  33.1 1.3 fusion.41
  34.4 2.2 reshape.295
  36.6 2.2 copy.31
  38.8 2.9 copy.30
  41.7 3.5 gather_fusion
  45.2 2.7 gather_fusion.1
  47.9 3.6 fusion.105
  51.6 0.8 subtract_convert_fusion
  52.4 0.5 copy-done.5
  52.9 1.5 bitcast_reduce_fusion
  54.5 1.2 fusion.106
  55.7 0.5 fusion.45
  56.3 1.9 fusion.14
  58.2 3.1 fusion.31
  61.3 0.6 fusion.43
  62.0 3.3 convolution_convert_fusion
  65.2 0.1 all-reduce.3.cloned.1.call-update
  65.3 0.1 all-reduce.5.cloned.1.call-start
  65.4 68.9 %all-reduce.3.cloned.1.call-done = bf16[16,64,2048]{2,1,0:T(8,128)(2,1)} async-done(((bf16[16,64,2048]{2,1,0:T(8,128)(2,1)}), bf16[16,64,2048]{2,1,0:T(8,128)(2,1)}) %all-reduce.3.cloned.1.call-update) | async-done | bytes 4194320 | tf_op jit(solution)/shard_map/psum | solution.py:70
  134.3 5.6 %fusion.9 = (f32[16,64]{1,0:T(8,128)S(1)}, bf16[16,64,2048]{2,1,0:T(8,128)(2,1)S(1)}) fusion(bf16[16,64,2048]{2,1,0:T(8,128)(2,1)} %all-reduce.3.cloned.1.call-done, bf16[16,64,2048]{2,1,0:T(8,128)(2,1)} %param.21), kind=kLoop, calls=%fused_computation.24 | loop fusion | flops 14679040 | bytes 12587008 | tf_op jit(solution)/shard_map/reduce_sum | solution.py:12
  140.0 2.0 copy-done.3
  142.0 6.4 %fusion.19 = f32[16,64,1024]{2,1,0:T(8,128)} fusion(bf16[2048,1024]{1,0:T(8,128)(2,1)S(1)} %copy-done.19, bf16[16,64,2048]{2,1,0:T(8,128)(2,1)S(1)} %get-tuple-element.12, f32[2048]{0:T(1024)S(1)} %convert_element_type.96, f32[16,64]{1,0:T(8,128)S(1)} %add_rsqrt_fusion.1), kind=kOutput, calls=%fused_computation.36 | convolution fusion | flops 4303355904 | bytes 12595200 | tf_op jit(solution)/shard_map/dot_general | solution.py:74
  148.3 15.6 %fusion.25 = bf16[16,64,2048]{2,1,0:T(8,128)(2,1)} fusion(bf16[1024,2048]{1,0:T(8,128)(2,1)} %param.37, f32[16,64,1024]{2,1,0:T(8,128)} %fusion.19, bf16[2048,1024]{1,0:T(8,128)(2,1)} %param.35, bf16[16,64,2048]{2,1,0:T(8,128)(2,1)} %copy-done.3, f32[2048]{0:T(1024)S(1)} %convert_element_type.96, f32[16,64]{1,0:T(8,128)S(1)} %add_rsqrt_fusion.1), kind=kOutput, calls=%fused_computation.44 | convolution fusion | flops 8606711808 | bytes 20983808 | tf_op jit(solution)/shard_map/dot_general | solution.py:76
  163.9 0.0 copy-start.18
  163.9 0.1 all-reduce.5.cloned.1.call-update
  164.0 0.6 copy-done.16
  164.6 0.0 copy-done.12
  164.7 0.1 reshape.338
  164.7 0.1 multiply_reduce_fusion
  164.8 0.1 and_reduce_fusion
  164.9 0.1 reshape.348
  165.0 0.1 pad_maximum_fusion.1
  165.1 0.2 copy.61
  165.2 6.1 %scatter_fusion.1 = bf16[6144,64]{1,0:T(8,128)(2,1)} fusion(bf16[6144,64]{1,0:T(8,128)(2,1)} %bitcast.142, s32[1024]{0:T(1024)S(1)} %reshape.348, bf16[1024,64]{1,0:T(8,128)(2,1)S(1)} %bitcast.150), kind=kCustom, calls=%fused_computation.5 | custom fusion | bytes 397312
  171.3 2.7 copy.46
  174.0 4.1 %scatter_fusion = bf16[6144,64]{1,0:T(8,128)(2,1)S(1)} fusion(bf16[6144,64]{1,0:T(8,128)(2,1)S(1)} %bitcast.139, s32[1024]{0:T(1024)S(1)} %reshape.348, bf16[1024,64]{1,0:T(8,128)(2,1)S(1)} %bitcast.148), kind=kCustom, calls=%fused_computation.4 | custom fusion | bytes 397312
  178.1 2.1 copy.45
  180.2 49.9 %all-reduce.5.cloned.1.call-done = bf16[16,64,2048]{2,1,0:T(8,128)(2,1)} async-done(((bf16[16,64,2048]{2,1,0:T(8,128)(2,1)}), bf16[16,64,2048]{2,1,0:T(8,128)(2,1)}) %all-reduce.5.cloned.1.call-update) | async-done | bytes 4194320 | tf_op jit(solution)/shard_map/psum | solution.py:76
  230.1 4.9 %fusion.2 = f32[16,64]{1,0:T(8,128)S(1)} fusion(bf16[16,64,2048]{2,1,0:T(8,128)(2,1)} %all-reduce.5.cloned.1.call-done, bf16[16,64,2048]{2,1,0:T(8,128)(2,1)} %copy-done.3), kind=kLoop, calls=%fused_computation.17 | loop fusion | flops 14679040 | bytes 8392704 | tf_op jit(solution)/shard_map/reduce_sum | solution.py:12
  235.0 84.0 %fusion.107 = (f32[16,64]{1,0:T(8,128)S(1)}, f32[16,64,16032]{2,1,0:T(8,128)}) fusion(bf16[2048,16032]{0,1:T(8,128)(2,1)} %param.39, f32[2048]{0:T(1024)S(1)} %convert_element_type.103, f32[16,64]{1,0:T(8,128)S(1)} %add_rsqrt_fusion, bf16[16,64,2048]{2,1,0:T(8,128)(2,1)} %all-reduce.5.cloned.1.call-done, bf16[16,64,2048]{2,1,0:T(8,128)(2,1)} %copy-done.3), kind=kOutput, calls=%fused_computation.149 | convolution fusion | flops 67276275712 | bytes 139739136 | tf_op jit(solution)/shard_map/dot_general | solution.py:78
  319.0 14.2 %pmax.7 = f32[16,64]{1,0:T(8,128)S(1)} all-reduce(f32[16,64]{1,0:T(8,128)S(1)} %get-tuple-element.29), channel_id=1, replica_groups=mesh['dp'=4,'tp'=8] {'tp'}, use_global_device_ids=true, to_apply=%region_10.11 | all-reduce | flops 1024 | bytes 8192 | tf_op jit(solution)/shard_map/pmax | solution.py:86
  333.2 16.4 %gather_fusion.2 = f32[1024]{0:T(1024)S(1)} fusion(f32[16,64,16032]{2,1,0:T(8,128)} %get-tuple-element.30, s32[1024]{0:T(1024)S(1)} %reshape.338), kind=kCustom, calls=%fused_computation.3 | custom fusion | bytes 20480 | tf_op jit(solution)/shard_map/jit(take_along_axis)/gather | solution.py:90
  349.6 20.9 %exponential_reduce_fusion = f32[16,64]{1,0:T(8,128)S(1)} fusion(f32[16,64,16032]{2,1,0:T(8,128)} %get-tuple-element.30, f32[16,64]{1,0:T(8,128)S(1)} %pmax.7), kind=kLoop, calls=%fused_computation.6 | loop fusion | flops 32832512 | bytes 65675264 | tf_op jit(solution)/shard_map/reduce_sum | solution.py:87
  370.6 0.1 gather.18
  370.7 23.6 %psum.23 = f32[2,16,64]{2,1,0:T(8,128)S(1)} all-reduce(f32[2,16,64]{2,1,0:T(8,128)S(1)} %pad_maximum_fusion.4), channel_id=1, replica_groups=mesh['dp'=4,'tp'=8] {'tp'}, use_global_device_ids=true, to_apply=%region_12.13 | all-reduce | flops 2048 | bytes 16384 | tf_op jit(solution)/shard_map/psum | solution.py:91
  394.3 0.6 fusion.84
  (57 shorter events, 0.2 us)
Async XLA Ops:
  7.2 54.8 %copy-start = (bf16[256,2048]{1,0:T(8,128)(2,1)S(1)}, bf16[256,2048]{1,0:T(8,128)(2,1)}, u32[]{:S(2)}) copy-start(bf16[256,2048]{1,0:T(8,128)(2,1)} %param.33) | copy-start | bytes 3145732
  7.2 7.0 %copy-start.2 = (s32[16,24]{1,0:T(8,128)S(1)}, s32[16,24]{1,0:T(8,128)}, u32[]{:S(2)}) copy-start(s32[16,24]{1,0:T(8,128)} %param.25) | copy-start | bytes 4612
  7.2 127.1 %all-reduce.3.cloned.1.call-start = ((), (), s32[]{:S(2)}) async-start(), calls=%async_computation | async-start | bytes 8388608 | tf_op jit(solution)/shard_map/psum | solution.py:70
  14.2 7.1 %copy-start.8 = (s32[16,64,64]{2,1,0:T(8,128)S(1)}, s32[16,64,64]{2,1,0:T(8,128)}, u32[]{:S(2)}) copy-start(s32[16,64,64]{2,1,0:T(8,128)} %param.22) | copy-start | bytes 786436
  14.2 7.5 %copy-start.21 = (bf16[2048,64]{0,1:T(8,128)(2,1)S(1)}, bf16[2048,64]{0,1:T(8,128)(2,1)}, u32[]{:S(2)}) copy-start(bf16[2048,64]{0,1:T(8,128)(2,1)} %param.32) | copy-start | bytes 786436
  21.7 4.4 %copy-start.4 = (bf16[16,64,2048]{2,1,0:T(8,128)(2,1)S(1)}, bf16[16,64,2048]{2,1,0:T(8,128)(2,1)}, u32[]{:S(2)}) copy-start(bf16[16,64,2048]{2,1,0:T(8,128)(2,1)} %param.21) | copy-start | bytes 12582916
  21.7 4.4 %copy-start.22 = (bf16[2048,64]{0,1:T(8,128)(2,1)S(1)}, bf16[2048,64]{0,1:T(8,128)(2,1)}, u32[]{:S(2)}) copy-start(bf16[2048,64]{0,1:T(8,128)(2,1)} %param.31) | copy-start | bytes 786436
  26.0 2.2 copy-start.13
  26.1 2.2 copy-start.14
  26.1 7.0 %copy-start.20 = (bf16[2048,256]{1,0:T(8,128)(2,1)S(1)}, bf16[2048,256]{1,0:T(8,128)(2,1)}, u32[]{:S(2)}) copy-start(bf16[2048,256]{1,0:T(8,128)(2,1)} %param.30) | copy-start | bytes 3145732
  47.9 3.6 copy-start.6
  51.5 1.4 copy-start.5
  51.5 1.4 copy-start.11
  55.7 2.5 copy-start.7
  58.2 3.1 copy-start.9
  62.0 3.4 copy-start.15
  65.3 164.7 %all-reduce.5.cloned.1.call-start = ((), (), s32[]{:S(2)}) async-start(), calls=%async_computation.1 | async-start | bytes 8388608 | tf_op jit(solution)/shard_map/psum | solution.py:76
  134.3 7.6 %copy-start.19 = (bf16[2048,1024]{1,0:T(8,128)(2,1)S(1)}, bf16[2048,1024]{1,0:T(8,128)(2,1)}, u32[]{:S(2)}) copy-start(bf16[2048,1024]{1,0:T(8,128)(2,1)} %param.36) | copy-start | bytes 12582916
  140.0 2.0 copy-start.3
  163.9 0.7 copy-start.16
  163.9 0.7 copy-start.12
  163.9 0.8 copy-start.10
  163.9 0.8 copy-start.18
  163.9 0.9 copy-start.17
  349.6 45.3 %copy-start.1 = (bf16[256,2048]{1,0:T(8,128)(2,1)S(1)}, bf16[256,2048]{1,0:T(8,128)(2,1)}, u32[]{:S(2)}) copy-start(bf16[256,2048]{1,0:T(8,128)(2,1)} %param.33) | copy-start | bytes 3145732
Sparse Core Ops, SparseCore 0:
  65.4 68.8 all-reduce.2
  164.1 65.8 all-reduce.4
where the time goes:
time: 411 us; the launch traced here: 402 us
  matrix products  124 us (30%)
  waiting for transfers between devices  119 us (29%)
  local copies, waits for them, and re-layouts  59.6 us (15%)
  other arithmetic  47.2 us (11%)
  blocking collectives  38.1 us (9%)
  between operations  14.9 us (4%)
    dot_general x1, matrix products, layer_and_logits(): jnp.dot(rms_norm(layer_out, final_norm), w_lm, preferred_element_type=jnp...  84 us
    psum x1, waiting for transfers between devices, layer_and_logits(): lax.psum(jnp.dot(attended, w_o, preferred_element_type=jnp.float32).astyp...  68.9 us
    psum x1, waiting for transfers between devices, layer_and_logits(): lax.psum(jnp.dot(product, w_down, preferred_element_type=jnp.float32).ast...  49.9 us
    psum x1, blocking collectives, group_step(): lax.psum(jnp.stack([part_sum, jnp.where(inside, picked, 0.0)]), 'tp')  23.9 us
    unnamed x55, local copies, waits for them, and re-layouts  23.3 us
    reduce_sum x1, other arithmetic, group_step(): part_sum = jnp.sum(jnp.exp(logits - global_top[..., None]), axis=-1)  20.9 us
    gather x3, local copies, waits for them, and re-layouts, group_step(): jnp.take_along_axis(logits, jnp.clip(local_id, 0, vocab_local - 1)[..., N...  16.5 us
    dot_general x1, matrix products, layer_and_logits(): jnp.dot(product, w_down, preferred_element_type=jnp.float32)  15.6 us
  transfers between devices with their start and end apart: 2, of which 2 were waited for; matrix products, arithmetic and copies ran while one was open for 4% of the time, Pallas kernels for 0%

commit v1 on v0

v1 whole, which is shorter than its diff:
```python
import functools

import jax
import jax.numpy as jnp
from jax import lax
from jax.experimental import pallas as pl
from jax.experimental.pallas import tpu as pltpu
from jax.sharding import PartitionSpec as P

RMS_EPS = 1e-5
ROPE_THETA = 500000
CHIPS = 4
CHUNKS = 2
TILE = 512
COLS = 512
STEP = 32
VMEM_LIMIT = 67043328
F32 = jnp.float32
BF16 = jnp.bfloat16


def rms_norm(values, gain):
    widened = values.astype(F32)
    scale = lax.rsqrt(jnp.mean(widened * widened, axis=-1, keepdims=True) + RMS_EPS)
    return (widened * scale * gain.astype(F32)).astype(BF16)


def rotate(values, positions):
    head_dim = values.shape[-1]
    half = head_dim // 2
    inv_freq = 1.0 / (ROPE_THETA ** (jnp.arange(half, dtype=F32) * (2.0 / head_dim)))
    angles = positions.astype(F32)[..., None] * inv_freq
    cosine = jnp.cos(angles)[..., None, :]
    sine = jnp.sin(angles)[..., None, :]
    first = values[..., :half]
    second = values[..., half:]
    return jnp.concatenate([first * cosine - second * sine, second * cosine + first * sine], axis=-1)


def tree_attention(query, key_new, val_new, key_old, val_old, tree_mask, ctx_len):
    scale = query.shape[-1] ** -0.5
    span = key_old.shape[1]
    score_old = jnp.einsum("btkgh,bskh->btkgs", query, key_old, preferred_element_type=F32) * scale
    seen_old = jnp.arange(span)[None, :] < ctx_len[:, None]
    score_old = jnp.where(seen_old[:, None, None, None, :], score_old, -jnp.inf)
    score_new = jnp.einsum("btkgh,bjkh->btkgj", query, key_new, preferred_element_type=F32) * scale
    score_new = jnp.where((tree_mask > 0)[:, :, None, None, :], score_new, -jnp.inf)
    top = jnp.maximum(jnp.max(score_old, axis=-1), jnp.max(score_new, axis=-1))[..., None]
    prob_old = jnp.exp(score_old - top)
    prob_new = jnp.exp(score_new - top)
    total = jnp.sum(prob_old, axis=-1) + jnp.sum(prob_new, axis=-1)
    mixed = jnp.einsum("btkgs,bskh->btkgh", prob_old.astype(BF16), val_old, preferred_element_type=F32)
    mixed = mixed + jnp.einsum("btkgj,bjkh->btkgh", prob_new.astype(BF16), val_new, preferred_element_type=F32)
    return (mixed / total[..., None]).astype(BF16)


def write_cache(cache, table, ctx_len, new_rows):
    page_size = cache.shape[1]
    slots = ctx_len[:, None] + jnp.arange(new_rows.shape[1])[None, :]
    slot_blocks = jnp.take_along_axis(table, slots // page_size, axis=1)
    return cache.at[slot_blocks, slots % page_size].set(new_rows)


class Copies:
    def __init__(self, make, plan):
        self.make = make
        self.plan = plan

    def __getitem__(self, k):
        return self.make(*self.plan[k]())

    def all(self):
        return [self[k] for k in range(len(self.plan))]


def tail_body(tp, att_hbm, hid_hbm, wo_hbm, wg_hbm, wu_hbm, wd_hbm, lm_hbm, gain_m, gain_f, target, norm_out, prob_out,
              att_own, att_far, hid, wo, wg, wu, wd, part, mrg_in, mrg_out, fin_in, h1, gat, fin, act, tiles, lga, lgb, run, stats,
              s_load, s_pair_s, s_pair_r, s_rs_s, s_rs_r, s_ag_s, s_ag_r, s_dd_s, s_dd_r, s_tile, s_st_s, s_st_r):
    me = lax.axis_index("tp")
    x = me // 2
    core = me % 2
    right = 2 * ((x + 1) % CHIPS) + core
    left = 2 * ((x + CHIPS - 1) % CHIPS) + core
    partner = me + 1 - 2 * core
    chunks, rows = h1.shape[0], h1.shape[1]
    half = rows // 2
    quad = CHIPS * rows
    wide = 2 * quad
    vocab = lm_hbm.shape[0]
    model = hid.shape[-1]

    def block(b, lo, n):
        return pl.ds(pl.multiple_of((b % CHIPS) * rows + lo, half), n)

    def remote(src, dst, ssem, rsem, dev):
        return pltpu.make_async_remote_copy(src_ref=src, dst_ref=dst, send_sem=ssem, recv_sem=rsem,
                                            device_id={"tp": dev}, device_id_type=pl.DeviceIdType.MESH)

    barrier = pltpu.get_barrier_semaphore()
    for k in range(1, tp):
        pl.semaphore_signal(barrier, inc=1, device_id={"tp": (me + k) % tp}, device_id_type=pl.DeviceIdType.MESH)

    def token_rows(p, c):
        return pl.ds(pl.multiple_of(p * wide + c * quad, quad), quad)

    loads = []

    def load(src, dst):
        loads.append(pltpu.make_async_copy(src, dst, s_load.at[len(loads)]))
        loads[-1].start()

    for p in range(chunks):
        load(att_hbm.at[token_rows(p, core)], att_own.at[p])
    load(wo_hbm, wo.at[0])
    for p in range(chunks):
        load(hid_hbm.at[pl.ds(pl.multiple_of(p * wide + core * quad + x * rows, rows), rows)], hid.at[p])
    load(wg_hbm, wg.at[0])
    load(wu_hbm, wu.at[0])
    load(wd_hbm, wd.at[0])

    pl.semaphore_wait(barrier, tp - 1)

    pair = []
    for src, dst in ([(att_hbm.at[token_rows(p, 1 - core)], att_far.at[p]) for p in range(chunks)] +
                     [(wo_hbm, wo.at[1]), (wg_hbm, wg.at[1]), (wu_hbm, wu.at[1]), (wd_hbm, wd.at[1])]):
        pair.append(remote(src, dst, s_pair_s.at[len(pair)], s_pair_r.at[len(pair)], partner))
        pair[-1].start()

    full, rest = vocab // TILE, vocab % TILE
    count = full + (1 if rest else 0)

    def tile_copy(p, i, size):
        slot = (p * count + i) % 3
        start = i * TILE if isinstance(i, int) else pl.multiple_of(i * TILE, TILE)
        return pltpu.make_async_copy(lm_hbm.at[pl.ds(start, size)], tiles.at[slot, pl.ds(0, size)], s_tile.at[slot])

    def size_of(i):
        return TILE if i < full else rest

    tile_copy(0, 0, TILE).start()
    tile_copy(0, 1, TILE).start()

    def project(p):
        @pl.loop(0, model // COLS)
        def _(n):
            cols = pl.ds(pl.multiple_of(n * COLS, COLS), COLS)
            acc = jnp.dot(att_own[p], wo[0, :, cols], preferred_element_type=F32)
            acc = acc + jnp.dot(att_far[p], wo[1, :, cols], preferred_element_type=F32)
            part[0, p, :, cols] = acc.astype(BF16)

    def rs_copies(ph, p):
        mine = part.at[ph, p]
        sem = lambda k: (s_rs_s.at[ph, p, k], s_rs_r.at[ph, p, k])
        top, low = pl.ds(0, half), pl.ds(half, half)
        plan = [
            lambda: (mine.at[block(x + 2, 0, half)], mrg_in.at[ph, p, 0], *sem(0), right),
            lambda: (mine.at[block(x + 2, half, half)], mrg_in.at[ph, p, 1], *sem(1), left),
            lambda: (mine.at[block(x + 1, half, half)], fin_in.at[ph, p, 0, low], *sem(2), right),
            lambda: (mine.at[block(x + 3, 0, half)], fin_in.at[ph, p, 1, top], *sem(3), left),
            lambda: (mrg_out.at[ph, p, 0], fin_in.at[ph, p, 0, top], *sem(4), right),
            lambda: (mrg_out.at[ph, p, 1], fin_in.at[ph, p, 1, low], *sem(5), left),
        ]
        return Copies(remote, plan)

    def rs_start(ph, p):
        for k in range(4):
            rs_copies(ph, p)[k].start()

    def rs_merge(ph, p):
        c = rs_copies(ph, p)
        c[0].wait_recv()
        mrg_out[ph, p, 0] = (part[ph, p, block(x + 1, 0, half), :].astype(F32) + mrg_in[ph, p, 0].astype(F32)).astype(BF16)
        c[4].start()
        c[1].wait_recv()
        mrg_out[ph, p, 1] = (part[ph, p, block(x + 3, half, half), :].astype(F32) + mrg_in[ph, p, 1].astype(F32)).astype(BF16)
        c[5].start()

    def rs_finish(ph, p):
        c = rs_copies(ph, p)
        for k in (2, 3, 4, 5):
            c[k].wait_recv()
        total = part[ph, p, block(x, 0, rows), :].astype(F32) + fin_in[ph, p, 0].astype(F32) + fin_in[ph, p, 1].astype(F32)
        return total.astype(BF16).astype(F32)

    def ag_copies(ph, p):
        if ph == 0:
            at = lambda b, lo: gat.at[p, block(b, lo, half)]
        else:
            at = lambda b, lo: fin.at[p, pl.ds(pl.multiple_of(core * quad + (b % CHIPS) * rows + lo, half), half)]
        sem = lambda k: (s_ag_s.at[ph, p, k], s_ag_r.at[ph, p, k])
        plan = [(x, 0, right), (x, half, right), (x, half, left), (x, 0, left), (x + 3, 0, right), (x + 1, half, left)]
        return Copies(remote, [lambda k=k, b=b, lo=lo, dev=dev: (at(b, lo), at(b, lo), *sem(k), dev) for k, (b, lo, dev) in enumerate(plan)])

    def dd_copies(p):
        def plan(k):
            at = fin.at[p, pl.ds(pl.multiple_of(core * quad + ((x + k) % CHIPS) * rows, rows), rows)]
            return at, at, s_dd_s.at[p, k], s_dd_r.at[p, k], partner

        return Copies(remote, [functools.partial(plan, k) for k in range(CHIPS)])

    def ag_start(ph, p):
        c = ag_copies(ph, p)
        for k in (0, 2, 1, 3):
            c[k].start()
        if ph == 1:
            dd_copies(p)[0].start()

    def ag_forward(ph, p):
        c = ag_copies(ph, p)
        c[0].wait_recv()
        c[4].start()
        c[2].wait_recv()
        c[5].start()

    def ag_wait(ph, p):
        c = ag_copies(ph, p)
        d = dd_copies(p)
        c[1].wait_recv()
        if ph == 1:
            d[3].start()
        c[3].wait_recv()
        if ph == 1:
            d[1].start()
        c[4].wait_recv()
        c[5].wait_recv()
        if ph == 1:
            d[2].start()

    def dd_wait(p):
        for d in dd_copies(p).all():
            d.wait_recv()

    def attn_end(p):
        summed = rs_finish(0, p)
        res = (hid[p].astype(F32) + summed).astype(BF16)
        h1[p] = res
        gat[p, block(x, 0, rows), :] = rms_norm(res, gain_m[...])
        ag_start(0, p)

    def mlp_end(p):
        summed = rs_finish(1, p)
        res = (h1[p].astype(F32) + summed).astype(BF16)
        fin[p, pl.ds(pl.multiple_of(core * quad + x * rows, rows), rows), :] = rms_norm(res, gain_f[...])
        ag_start(1, p)

    def mlp(p):
        ffn = wg.shape[-1]
        for s in range(2):
            @pl.loop(0, ffn // COLS)
            def _(n):
                cols = pl.ds(pl.multiple_of(n * COLS, COLS), COLS)
                gate = jnp.dot(gat[p], wg[s, :, cols], preferred_element_type=F32)
                upper = jnp.dot(gat[p], wu[s, :, cols], preferred_element_type=F32)
                act[s, :, cols] = (jax.nn.silu(gate) * upper).astype(BF16)

        @pl.loop(0, model // COLS)
        def _(n):
            cols = pl.ds(pl.multiple_of(n * COLS, COLS), COLS)
            acc = jnp.dot(act[0], wd[0, :, cols], preferred_element_type=F32)
            acc = acc + jnp.dot(act[1], wd[1, :, cols], preferred_element_type=F32)
            part[1, p, :, cols] = acc.astype(BF16)

    def multiply(p, i, size, out):
        slot = (p * count + i) % 3
        tile_copy(p, i, size).wait()
        out[pl.ds(0, size), :] = lax.dot_general(tiles[slot, pl.ds(0, size), :], fin[p], (((1,), (1,)), ((), ())),
                                                 preferred_element_type=F32)

    def fold(p, i, size, src):
        goal = target[p] - (me * vocab + i * TILE) - lax.broadcasted_iota(jnp.int32, (8, wide), 0)
        depth = STEP // 8
        offsets = 8 * lax.broadcasted_iota(jnp.int32, (depth, 8, wide), 0)
        old = run[0]
        top = old
        for r in range(0, size, STEP):
            top = jnp.maximum(top, jnp.max(src[pl.ds(r, STEP), :].reshape(depth, 8, wide), axis=0))
        total = run[1] * jnp.exp(old - top)
        chosen = run[2]
        for r in range(0, size, STEP):
            piece = src[pl.ds(r, STEP), :].reshape(depth, 8, wide)
            total = total + jnp.sum(jnp.exp(piece - top[None]), axis=0)
            chosen = chosen + jnp.sum(jnp.where((goal - r)[None] == offsets, piece, 0.0), axis=0)
        run[0] = top
        run[1] = total
        run[2] = chosen

    def head(p, events):
        run[0] = jnp.full(run.shape[1:], -jnp.inf, F32)
        run[1] = jnp.zeros(run.shape[1:], F32)
        run[2] = jnp.zeros(run.shape[1:], F32)
        tile_copy(p, 2, TILE).start()
        multiply(p, 0, TILE, lga)

        def pairs(lo, hi):
            if lo >= hi:
                return

            @pl.loop(lo, hi)
            def _(j):
                i = 2 * j
                tile_copy(p, i + 3, TILE).start()
                multiply(p, i + 1, TILE, lgb)
                fold(p, i, TILE, lga)
                tile_copy(p, i + 4, TILE).start()
                multiply(p, i + 2, TILE, lga)
                fold(p, i + 1, TILE, lgb)

        loops = (full - 4) // 2
        cuts = sorted(set([0, loops] + [min(e[0], loops) for e in events]))
        for e in events:
            if e[0] == 0:
                e[1]()
        for lo, hi in zip(cuts[:-1], cuts[1:]):
            pairs(lo, hi)
            for e in events:
                if min(e[0], loops) == hi and e[0] > 0:
                    e[1]()
        done = 2 * loops
        bufs = (lga, lgb)
        for i in range(done, count):
            nxt = i + 3
            if nxt < count:
                tile_copy(p, nxt, size_of(nxt)).start()
            elif p + 1 < chunks and nxt - count < 2:
                tile_copy(p + 1, nxt - count, TILE).start()
            if i + 1 < count:
                multiply(p, i + 1, size_of(i + 1), bufs[(i + 1) % 2])
            fold(p, i, size_of(i), bufs[i % 2])
        top = jnp.max(run[0], axis=0, keepdims=True)
        total = jnp.sum(run[1] * jnp.exp(run[0] - top), axis=0, keepdims=True)
        chosen = jnp.sum(run[2], axis=0, keepdims=True)
        for k, row in enumerate((top, total, chosen)):
            for g in range(wide // 128):
                stats[me, k, pl.ds(p * (wide // 128) + g, 1), :] = row[:, g * 128:(g + 1) * 128]

    def wait_loads(lo, hi):
        for k in range(lo, hi):
            loads[k].wait()

    wait_loads(0, chunks + 1)
    for k in range(chunks):
        pair[k].wait_recv()
    pair[chunks].wait_recv()
    for p in range(chunks):
        project(p)
        rs_start(0, p)
    wait_loads(chunks + 1, 2 * chunks + 1)
    for p in range(chunks):
        rs_merge(0, p)
    attn_end(0)
    attn_end(1)
    ag_forward(0, 0)
    ag_forward(0, 1)
    wait_loads(2 * chunks + 1, len(loads))
    for k in (1, 2, 3):
        pair[chunks + k].wait_recv()
    for p in range(chunks):
        ag_wait(0, p)
        mlp(p)
        rs_start(1, p)
    rs_merge(1, 0)
    mlp_end(0)
    rs_merge(1, 1)
    mlp_end(1)
    ag_forward(1, 0)
    ag_wait(1, 0)
    dd_wait(0)
    head(0, [(2, lambda: ag_forward(1, 1)), (6, lambda: ag_wait(1, 1))])
    dd_wait(1)
    head(1, [])

    sent = []
    for k in range(1, tp):
        sent.append(remote(stats.at[me], stats.at[me], s_st_s.at[k - 1], s_st_r.at[k - 1], (me + k) % tp))
        sent[-1].start()
    for d in sent:
        d.wait_recv()
    top = stats[0, 0]
    for k in range(1, tp):
        top = jnp.maximum(top, stats[k, 0])
    total = jnp.zeros_like(top)
    chosen = jnp.zeros_like(top)
    for k in range(tp):
        total = total + stats[k, 1] * jnp.exp(stats[k, 0] - top)
        chosen = chosen + stats[k, 2]
    log_norm = top + jnp.log(total)
    norm_out[...] = log_norm
    prob_out[...] = chosen - log_norm

    for d in sent + pair:
        d.wait_send()
    for p in range(chunks):
        for ph in range(2):
            for d in rs_copies(ph, p).all() + ag_copies(ph, p).all():
                d.wait_send()
        for d in dd_copies(p).all():
            d.wait_send()


def tail(tp, attended, hidden, w_o, w_gate, w_up, w_down, w_lm, mlp_norm, final_norm, score_id):
    tokens, model = hidden.shape
    heads = attended.shape[-1]
    ffn = w_gate.shape[-1]
    rows = tokens // (CHUNKS * tp)
    quad = CHIPS * rows
    wide = 2 * quad
    target = jnp.broadcast_to(score_id.reshape(CHUNKS, 1, wide), (CHUNKS, 8, wide))
    anyspace = pl.BlockSpec(memory_space=pl.ANY)
    vmem = pl.BlockSpec(memory_space=pltpu.VMEM)
    dma = pltpu.SemaphoreType.DMA
    flops = 2 * tokens * model * (w_lm.shape[-1] + 3 * ffn + heads)
    log_norm, log_prob = pl.pallas_call(
        functools.partial(tail_body, tp),
        out_shape=[jax.ShapeDtypeStruct((tokens // 128, 128), F32)] * 2,
        in_specs=[anyspace] * 7 + [vmem] * 3,
        out_specs=[vmem] * 2,
        scratch_shapes=[
            pltpu.VMEM((CHUNKS, quad, heads), BF16), pltpu.VMEM((CHUNKS, quad, heads), BF16),
            pltpu.VMEM((CHUNKS, rows, model), BF16), pltpu.VMEM((2, heads, model), BF16),
            pltpu.VMEM((2, model, ffn), BF16), pltpu.VMEM((2, model, ffn), BF16), pltpu.VMEM((2, ffn, model), BF16),
            pltpu.VMEM((2, CHUNKS, quad, model), BF16), pltpu.VMEM((2, CHUNKS, 2, rows // 2, model), BF16),
            pltpu.VMEM((2, CHUNKS, 2, rows // 2, model), BF16), pltpu.VMEM((2, CHUNKS, 2, rows, model), BF16),
            pltpu.VMEM((CHUNKS, rows, model), BF16), pltpu.VMEM((CHUNKS, quad, model), BF16),
            pltpu.VMEM((CHUNKS, wide, model), BF16), pltpu.VMEM((2, quad, ffn), BF16),
            pltpu.VMEM((3, TILE, model), BF16), pltpu.VMEM((TILE, wide), F32), pltpu.VMEM((TILE, wide), F32),
            pltpu.VMEM((3, 8, wide), F32), pltpu.VMEM((tp, 3, tokens // 128, 128), F32),
            dma((2 * CHUNKS + 4,)), dma((CHUNKS + 4,)), dma((CHUNKS + 4,)),
            dma((2, CHUNKS, 6)), dma((2, CHUNKS, 6)), dma((2, CHUNKS, 6)), dma((2, CHUNKS, 6)),
            dma((CHUNKS, CHIPS)), dma((CHUNKS, CHIPS)), dma((3,)), dma((tp - 1,)), dma((tp - 1,)),
        ],
        compiler_params=pltpu.CompilerParams(collective_id=0, has_side_effects=True, vmem_limit_bytes=VMEM_LIMIT),
        cost_estimate=pl.CostEstimate(flops=flops, bytes_accessed=2 * CHUNKS * w_lm.size, transcendentals=tokens * w_lm.shape[-1]),
        name="layer_tail_and_head",
    )(attended, hidden, w_o, w_gate, w_up, w_down, w_lm.T, mlp_norm.reshape(1, -1), final_norm.reshape(1, -1), target)
    return log_norm, log_prob


def solution(mesh):
    tp = mesh.shape["tp"]

    def group_step(hidden, tree_mask, depth, ctx_len, block_table, score_id, k_cache, v_cache, attn_norm, w_q, w_k, w_v, w_o, mlp_norm, w_gate, w_up, w_down, final_norm, w_lm):
        requests, nodes, model = hidden.shape
        page_size, kv_local, head_dim = k_cache.shape[1:]
        span = block_table.shape[1] * page_size
        heads_local = w_q.shape[1] // head_dim
        normed = rms_norm(hidden, attn_norm)
        positions = ctx_len[:, None] + depth
        query = jnp.dot(normed, w_q, preferred_element_type=F32).reshape(requests, nodes, heads_local, head_dim)
        query = rotate(query, positions).astype(BF16).reshape(requests, nodes, kv_local, heads_local // kv_local, head_dim)
        key_new = jnp.dot(normed, w_k, preferred_element_type=F32).reshape(requests, nodes, kv_local, head_dim)
        key_new = rotate(key_new, positions).astype(BF16)
        val_new = jnp.dot(normed, w_v, preferred_element_type=F32).astype(BF16).reshape(requests, nodes, kv_local, head_dim)
        key_old = k_cache[block_table].reshape(requests, span, kv_local, head_dim)
        val_old = v_cache[block_table].reshape(requests, span, kv_local, head_dim)
        attended = tree_attention(query, key_new, val_new, key_old, val_old, tree_mask, ctx_len)
        attended = attended.reshape(requests * nodes, heads_local * head_dim)
        log_norm, log_prob = tail(tp, attended, hidden.reshape(requests * nodes, model), w_o, w_gate, w_up, w_down, w_lm, mlp_norm, final_norm, score_id)
        return (log_norm.reshape(requests, nodes), log_prob.reshape(requests, nodes),
                write_cache(k_cache, block_table, ctx_len, key_new), write_cache(v_cache, block_table, ctx_len, val_new))

    request_spec = P("dp", None, None)
    node_spec = P("dp", None)
    cache_spec = P("dp", None, "tp", None)
    shared_spec = P(None)
    column_spec = P(None, "tp")
    row_spec = P("tp", None)
    in_specs = (request_spec, request_spec, node_spec, P("dp"), node_spec, node_spec, cache_spec, cache_spec, shared_spec, column_spec, column_spec, column_spec, row_spec, shared_spec, column_spec, column_spec, row_spec, shared_spec, column_spec)
    out_specs = (node_spec, node_spec, cache_spec, cache_spec)
    return jax.shard_map(group_step, mesh=mesh, in_specs=in_specs, out_specs=out_specs, check_vma=False)
```

time: 411 us -> 275 us (0.67)
  the two profiles are of different devices: /device:TPU:80 before, /device:TPU:81 now
where the time goes in v1:
time: 275 us; the launch traced here: 271 us
  Pallas kernels  194 us (71%)
  local copies, waits for them, and re-layouts  41.7 us (15%)
  matrix products  17.1 us (6%)
  other arithmetic  16.1 us (6%)
    pallas_call x1, Pallas kernels, tail(): pl.pallas_call(functools.partial(tail_body, tp), out_shape=[jax.ShapeDtyp...  194 us
    unnamed x59, local copies, waits for them, and re-layouts  18.5 us
    gather x3, local copies, waits for them, and re-layouts, write_cache(): slot_blocks = jnp.take_along_axis(table, slots // page_size, axis=1)  7.35 us

profile of v1, /device:TPU:81, one launch (start us, length us, event | category | flops | bytes accessed | tf_op | source)
XLA Modules:
  0.0 270.6 jit_solution(5355482227355546288)
XLA Ops:
  0.6 0.0 copy-start.8
  0.7 3.2 %fusion = f32[16,64]{1,0:T(8,128)S(1)} fusion(bf16[16,64,2048]{2,1,0:T(8,128)(2,1)} %param.21), kind=kLoop, calls=%fused_computation.7 | loop fusion | flops 6290432 | bytes 4198400 | tf_op jit(solution)/shard_map/reduce_sum | solution.py:24
  3.9 0.2 copy-done.8
  4.1 2.5 fusion.17
  6.6 0.9 reshape.270
  7.5 0.0 copy-start.18
  7.5 3.3 %fusion.59 = (f32[16,64,4,32]{3,2,1,0:T(4,128)}, f32[16,64,4,32]{3,2,1,0:T(4,128)}) fusion(f32[16,64,4,64]{3,2,1,0:T(4,128)S(1)} %reshape.270), kind=kLoop, calls=%fused_computation.96 | loop fusion | bytes 2097152 | tf_op jit(solution)/shard_map/slice | solution.py:35
  10.8 0.7 bitcast_or_fusion
  11.5 0.1 reshape.356
  11.6 7.2 %gather_fusion.2 = s32[1024]{0:T(1024)S(1)} fusion(s32[16,24]{1,0:T(8,128)S(1)} %copy-done, s32[1024]{0:T(1024)S(1)} %reshape.356), kind=kCustom, calls=%fused_computation.clone | custom fusion | bytes 16384 | tf_op jit(solution)/shard_map/jit(take_along_axis)/gather | solution.py:60
  18.8 0.1 reshape.359
  18.9 0.7 fusion.49
  19.5 1.9 multiply_cosine_fusion
  21.4 0.0 copy-start.9
  21.4 0.0 copy-start.24
  21.5 3.2 %subtract_convert_fusion = (bf16[16,64,4,32]{3,1,2,0:T(8,128)(2,1)S(1)}, bf16[16,64,4,32]{3,1,2,0:T(8,128)(2,1)S(1)}) fusion(f32[16,64,4,32]{3,2,1,0:T(4,128)} %get-tuple-element.16, f32[16,64,4,32]{3,2,1,0:T(4,128)} %get-tuple-element.15, f32[16,64,32]{2,1,0:T(8,128)S(1)} %get-tuple-element.20, f32[16,64,32]{2,1,0:T(8,128)S(1)} %get-tuple-element.19), kind=kLoop, calls=%fused_computation.30 | loop fusion | flops 1048576 | bytes 1835008 | tf_op jit(solution)/shard_map/convert.6
  24.6 0.0 copy-start.5
  24.7 0.2 copy-done.9
  24.9 0.0 copy-done.24
  24.9 2.2 fusion.23
  27.1 1.2 fusion.38
  28.3 0.0 copy-start.12
  28.3 0.1 broadcast_compare_fusion
  28.4 0.3 copy.35
  28.7 0.0 copy-start.13
  28.7 2.5 fusion.60
  31.3 1.3 copy.31
  32.6 0.0 copy-start.1
  32.6 0.1 reshape.299
  32.7 2.6 gather_fusion.1
  35.2 0.1 iota_compare_fusion
  35.3 3.3 %bitcast_reduce_fusion = (f32[16,64,4]{1,2,0:T(4,128)S(1)}, f32[16,384,64,4]{1,2,3,0:T(8,128)S(1)}) fusion(pred[16,384]{1,0:T(8,128)(4,1)S(1)} %iota_compare_fusion, bf16[16,384,64,1]{2,1,3,0:T(8,128)(2,1)} %bitcast.104, bf16[16,64,4,32]{3,1,2,0:T(8,128)(2,1)} %copy-done.5, bf16[16,64,4,32]{3,1,2,0:T(8,128)(2,1)S(1)} %get-tuple-element.13), kind=kOutput, calls=%fused_computation.11 | convolution fusion | flops 207089664 | bytes 7624704 | tf_op jit(solution)/shard_map/btkgh,bskh->btkgs/dot_general | solution.py:43
  38.7 0.0 copy-done.1
  38.7 0.0 copy-start.4
  38.7 0.6 fusion.20
  39.3 1.9 fusion.4
  41.2 0.2 copy-done.4
  41.4 1.3 copy.30
  42.7 1.9 gather_fusion
  44.6 0.0 copy-start.10
  44.6 0.0 copy-start.25
  44.6 4.5 %fusion.7 = f32[16,64,64,4]{2,1,3,0:T(8,128)S(1)} fusion(bf16[16,384,64,1]{2,1,3,0:T(8,128)(2,1)S(1)} %bitcast.106, f32[16,384,64,4]{1,2,3,0:T(8,128)} %copy-done.4, f32[16,64,4]{1,2,0:T(4,128)S(1)} %max.9, pred[16,384]{1,0:T(8,128)(4,1)S(1)} %iota_compare_fusion), kind=kOutput, calls=%fused_computation.17 | convolution fusion | flops 207618048 | bytes 8148992 | tf_op jit(solution)/shard_map/btkgs,bskh->btkgh/dot_general | solution.py:52
  49.2 1.3 fusion.26
  50.5 0.3 copy-done.7
  50.8 0.7 fusion.22
  51.5 0.0 copy-done.16
  51.5 0.7 copy.40
  52.2 1.5 reshape.274.att_hbm
  53.7 0.1 broadcast_in_dim.39
  53.8 0.6 broadcast_in_dim.40.target
  54.4 0.6 reshape.276.gain_m
  55.0 0.6 reshape.277.gain_f
  55.6 194.3 %layer_tail_and_head.1 = (f32[8,128]{1,0:T(8,128)}, f32[8,128]{1,0:T(8,128)}) custom-call(bf16[1024,256]{1,0:T(8,128)(2,1)} %reshape.274.att_hbm, bf16[1024,2048]{1,0:T(8,128)(2,1)} %bitcast.105, bf16[256,2048]{1,0:T(8,128)(2,1)} %wo_hbm.1, bf16[2048,1024]{1,0:T(8,128)(2,1)} %wg_hbm.1, bf16[2048,1024]{1,0:T(8,128)(2,1)} %wu_hbm.1, ...), custom_call_target="tpu_custom_call" | custom-call | flops 81201725440 | bytes 131334144 | tf_op jit(solution)/shard_map/layer_tail_and_head/pallas_call | solution.py:412
  249.9 1.3 reshape.278
  251.3 1.3 reshape.279
  252.6 1.0 pad_maximum_fusion.1
  253.7 0.2 copy.60
  253.8 0.8 multiply_reduce_fusion
  254.6 0.8 and_reduce_fusion
  255.4 0.1 reshape.319
  255.5 6.0 %scatter_fusion = bf16[6144,64]{1,0:T(8,128)(2,1)} fusion(bf16[6144,64]{1,0:T(8,128)(2,1)} %bitcast.99, s32[1024]{0:T(1024)S(1)} %reshape.319, bf16[1024,64]{1,0:T(8,128)(2,1)S(1)} %bitcast.109), kind=kCustom, calls=%fused_computation.3 | custom fusion | bytes 397312
  261.5 2.8 %copy.45 = bf16[384,16,1,64]{0,3,2,1:T(8,128)(2,1)} copy(bf16[384,16,1,64]{3,1,0,2:T(8,128)(2,1)} %bitcast.100) | data formatting | bytes 1572864
  264.4 4.1 %scatter_fusion.1 = bf16[6144,64]{1,0:T(8,128)(2,1)S(1)} fusion(bf16[6144,64]{1,0:T(8,128)(2,1)S(1)} %bitcast.102, s32[1024]{0:T(1024)S(1)} %reshape.319, bf16[1024,64]{1,0:T(8,128)(2,1)S(1)} %bitcast.110), kind=kCustom, calls=%fused_computation.4 | custom fusion | bytes 397312
  268.5 1.9 copy.46
  (42 shorter events, 0.1 us)
Async XLA Ops:
  0.6 3.5 %copy-start.8 = (bf16[16,64,2048]{2,1,0:T(8,128)(2,1)S(1)}, bf16[16,64,2048]{2,1,0:T(8,128)(2,1)}, u32[]{:S(2)}) copy-start(bf16[16,64,2048]{2,1,0:T(8,128)(2,1)} %param.21) | copy-start | bytes 12582916
  0.6 3.3 %copy-start.21 = (bf16[2048]{0:T(1024)(128)(2,1)S(1)}, bf16[2048]{0:T(1024)(128)(2,1)}, u32[]{:S(2)}) copy-start(bf16[2048]{0:T(1024)(128)(2,1)} %param.29) | copy-start | bytes 12292
  7.5 3.3 %copy-start.18 = (s32[16]{0:T(128)S(1)}, s32[16]{0:T(128)}, u32[]{:S(2)}) copy-start(s32[16]{0:T(128)} %param.24) | copy-start | bytes 196
  10.8 0.8 copy-start
  11.6 7.3 %copy-start.20 = (s32[16,64]{1,0:T(8,128)S(1)}, s32[16,64]{1,0:T(8,128)}, u32[]{:S(2)}) copy-start(s32[16,64]{1,0:T(8,128)} %param.23) | copy-start | bytes 12292
  21.4 3.5 %copy-start.9 = (bf16[16,64,2048]{2,1,0:T(8,128)(2,1)S(1)}, bf16[16,64,2048]{2,1,0:T(8,128)(2,1)}, u32[]{:S(2)}) copy-start(bf16[16,64,2048]{2,1,0:T(8,128)(2,1)} %param.21) | copy-start | bytes 12582916
  21.4 3.5 %copy-start.24 = (bf16[2048,64]{0,1:T(8,128)(2,1)S(1)}, bf16[2048,64]{0,1:T(8,128)(2,1)}, u32[]{:S(2)}) copy-start(bf16[2048,64]{0,1:T(8,128)(2,1)} %param.31) | copy-start | bytes 786436
  24.6 6.6 %copy-start.5 = (bf16[16,64,4,32]{3,1,2,0:T(8,128)(2,1)}, bf16[16,64,4,32]{3,1,2,0:T(8,128)(2,1)S(1)}, u32[]{:S(2)}) copy-start(bf16[16,64,4,32]{3,1,2,0:T(8,128)(2,1)S(1)} %get-tuple-element.14) | copy-start | bytes 786436
  24.9 3.4 %copy-start.15 = (s32[16,64,64]{2,1,0:T(8,128)S(1)}, s32[16,64,64]{2,1,0:T(8,128)}, u32[]{:S(2)}) copy-start(s32[16,64,64]{2,1,0:T(8,128)} %param.22) | copy-start | bytes 786436
  28.3 2.9 %copy-start.11 = (bf16[16,64,1,32]{1,3,0,2:T(8,128)(2,1)}, bf16[16,64,1,32]{1,3,0,2:T(8,128)(2,1)S(1)}, u32[]{:S(2)}) copy-start(bf16[16,64,1,32]{1,3,0,2:T(8,128)(2,1)S(1)} %get-tuple-element.17) | copy-start | bytes 196612
  28.3 2.9 %copy-start.12 = (bf16[16,64,1,32]{1,3,0,2:T(8,128)(2,1)}, bf16[16,64,1,32]{1,3,0,2:T(8,128)(2,1)S(1)}, u32[]{:S(2)}) copy-start(bf16[16,64,1,32]{1,3,0,2:T(8,128)(2,1)S(1)} %get-tuple-element.18) | copy-start | bytes 196612
  28.7 2.6 copy-start.13
  32.6 6.1 %copy-start.1 = (bf16[384,16,1,64]{3,1,0,2:T(8,128)(2,1)}, bf16[384,16,1,64]{3,1,0,2:T(8,128)(2,1)S(1)}, u32[]{:S(2)}) copy-start(bf16[384,16,1,64]{3,1,0,2:T(8,128)(2,1)S(1)} %copy.31) | copy-start | bytes 2359300
  35.3 3.4 %copy-start.6 = (f32[16,64,1,4,64]{1,4,3,0,2:T(8,128)S(1)}, f32[16,64,1,4,64]{1,4,3,0,2:T(8,128)}, u32[]{:S(2)}) copy-start(f32[16,64,1,4,64]{1,4,3,0,2:T(8,128)} %get-tuple-element.28) | copy-start | bytes 3145732
  38.7 2.7 copy-start.4
  39.3 2.1 copy-start.14
  42.7 6.5 %copy-start.2 = (bf16[384,16,1,64]{3,1,0,2:T(8,128)(2,1)}, bf16[384,16,1,64]{3,1,0,2:T(8,128)(2,1)S(1)}, u32[]{:S(2)}) copy-start(bf16[384,16,1,64]{3,1,0,2:T(8,128)(2,1)S(1)} %copy.30) | copy-start | bytes 2359300
  44.6 4.6 %copy-start.10 = (bf16[16,64,2048]{2,1,0:T(8,128)(2,1)S(1)}, bf16[16,64,2048]{2,1,0:T(8,128)(2,1)}, u32[]{:S(2)}) copy-start(bf16[16,64,2048]{2,1,0:T(8,128)(2,1)} %param.21) | copy-start | bytes 12582916
  44.6 4.6 %copy-start.25 = (bf16[2048,64]{0,1:T(8,128)(2,1)S(1)}, bf16[2048,64]{0,1:T(8,128)(2,1)}, u32[]{:S(2)}) copy-start(bf16[2048,64]{0,1:T(8,128)(2,1)} %param.32) | copy-start | bytes 786436
  49.2 1.6 copy-start.7
  50.8 0.7 copy-start.16
  51.5 2.2 copy-start.19
  51.5 2.9 %copy-start.22 = (bf16[2048]{0:T(1024)(128)(2,1)S(1)}, bf16[2048]{0:T(1024)(128)(2,1)}, u32[]{:S(2)}) copy-start(bf16[2048]{0:T(1024)(128)(2,1)} %param.34) | copy-start | bytes 12292
  51.5 3.5 %copy-start.23 = (bf16[2048]{0:T(1024)(128)(2,1)S(1)}, bf16[2048]{0:T(1024)(128)(2,1)}, u32[]{:S(2)}) copy-start(bf16[2048]{0:T(1024)(128)(2,1)} %param.38) | copy-start | bytes 12292
  261.5 2.8 %copy-start.3 = (bf16[384,16,1,64]{3,1,0,2:T(8,128)(2,1)S(1)}, bf16[384,16,1,64]{3,1,0,2:T(8,128)(2,1)}, u32[]{:S(2)}) copy-start(bf16[384,16,1,64]{3,1,0,2:T(8,128)(2,1)} %copy-done.2) | copy-start | bytes 2359300
  261.5 2.8 %copy-start.17 = (bf16[16,64,64]{2,1,0:T(8,128)(2,1)S(1)}, bf16[16,64,64]{2,1,0:T(8,128)(2,1)}, u32[]{:S(2)}) copy-start(bf16[16,64,64]{2,1,0:T(8,128)(2,1)} %copy-done.16) | copy-start | bytes 393220

commit v2 on v1

--- a/solution.py
+++ b/solution.py
@@ -10,6 +10,7 @@
 RMS_EPS = 1e-5
 ROPE_THETA = 500000
 CHIPS = 4
+PER_STEP = 4
 CHUNKS = 2
 TILE = 512
 COLS = 512
@@ -25,40 +26,113 @@
     return (widened * scale * gain.astype(F32)).astype(BF16)
 
 
-def rotate(values, positions):
-    head_dim = values.shape[-1]
-    half = head_dim // 2
-    inv_freq = 1.0 / (ROPE_THETA ** (jnp.arange(half, dtype=F32) * (2.0 / head_dim)))
-    angles = positions.astype(F32)[..., None] * inv_freq
-    cosine = jnp.cos(angles)[..., None, :]
-    sine = jnp.sin(angles)[..., None, :]
-    first = values[..., :half]
-    second = values[..., half:]
-    return jnp.concatenate([first * cosine - second * sine, second * cosine + first * sine], axis=-1)
-
-
-def tree_attention(query, key_new, val_new, key_old, val_old, tree_mask, ctx_len):
-    scale = query.shape[-1] ** -0.5
-    span = key_old.shape[1]
-    score_old = jnp.einsum("btkgh,bskh->btkgs", query, key_old, preferred_element_type=F32) * scale
-    seen_old = jnp.arange(span)[None, :] < ctx_len[:, None]
-    score_old = jnp.where(seen_old[:, None, None, None, :], score_old, -jnp.inf)
-    score_new = jnp.einsum("btkgh,bjkh->btkgj", query, key_new, preferred_element_type=F32) * scale
-    score_new = jnp.where((tree_mask > 0)[:, :, None, None, :], score_new, -jnp.inf)
-    top = jnp.maximum(jnp.max(score_old, axis=-1), jnp.max(score_new, axis=-1))[..., None]
-    prob_old = jnp.exp(score_old - top)
-    prob_new = jnp.exp(score_new - top)
-    total = jnp.sum(prob_old, axis=-1) + jnp.sum(prob_new, axis=-1)
-    mixed = jnp.einsum("btkgs,bskh->btkgh", prob_old.astype(BF16), val_old, preferred_element_type=F32)
-    mixed = mixed + jnp.einsum("btkgj,bjkh->btkgh", prob_new.astype(BF16), val_new, preferred_element_type=F32)
-    return (mixed / total[..., None]).astype(BF16)
-
-
-def write_cache(cache, table, ctx_len, new_rows):
-    page_size = cache.shape[1]
-    slots = ctx_len[:, None] + jnp.arange(new_rows.shape[1])[None, :]
-    slot_blocks = jnp.take_along_axis(table, slots // page_size, axis=1)
-    return cache.at[slot_blocks, slots % page_size].set(new_rows)
+def attention_body(per, pages, ctx, table, hidden, gain, w_q, w_k, w_v, cosine, sine, mask, k_in, v_in, att, k_out, v_out, w_kv, q_heads, k_old, v_old):
+    step = pl.program_id(0)
+    nodes = mask.shape[1]
+    size = k_in.shape[1]
+    dim = k_in.shape[2]
+    heads = w_q.shape[1] // dim
+    span = pages * size
+    lanes = 2 * dim
+
+    @pl.when(step == 0)
+    def _():
+        w_kv[pl.ds(0, dim), :] = w_k[...]
+        w_kv[pl.ds(dim, dim), :] = w_v[...]
+        k_out[...] = k_in[...]
+        v_out[...] = v_in[...]
+
+    normed = rms_norm(hidden[...], gain[...])
+    queries = jnp.dot(normed, w_q[...], preferred_element_type=F32)
+    pair = lax.dot_general(normed, w_kv[...], (((1,), (1,)), ((), ())), preferred_element_type=F32)
+    lane = lax.broadcasted_iota(jnp.int32, (per * nodes, lanes), 1)
+    lower = (lane % dim) < dim // 2
+
+    def rotate(values):
+        swapped = jnp.where(lower, pltpu.roll(values, lanes - dim // 2, 1), pltpu.roll(values, dim // 2, 1))
+        return values * cosine[...] + swapped * sine[...]
+
+    for h in range(0, heads, 2):
+        turned = rotate(queries[:, h * dim:(h + 2) * dim]).astype(BF16)
+        q_heads[h] = turned[:, :dim]
+        q_heads[h + 1] = turned[:, dim:]
+    pair = jnp.where(lane < dim, rotate(pair), pair).astype(BF16)
+    scale = dim ** -0.5
+    slot = lax.broadcasted_iota(jnp.int32, (heads * nodes, span), 1)
+    row = lax.broadcasted_iota(jnp.int32, (size, dim), 0)
+    for r in range(per):
+        b = step * per + r
+        length = ctx[b]
+        for j in range(pages):
+            page = table[b * pages + j]
+            k_old[r, pl.ds(j * size, size), :] = k_in[page]
+            v_old[r, pl.ds(j * size, size), :] = v_in[page]
+        own = slice(r * nodes, (r + 1) * nodes)
+        fresh = pair[own]
+        k_new = fresh[:, :dim]
+        v_new = fresh[:, dim:]
+        query = q_heads[:, pl.ds(r * nodes, nodes), :].reshape(heads * nodes, dim)
+        nt = (((1,), (1,)), ((), ()))
+        score_old = lax.dot_general(query, k_old[r], nt, preferred_element_type=F32) * scale
+        score_old = jnp.where(slot < length, score_old, -jnp.inf)
+        score_new = lax.dot_general(query, k_new, nt, preferred_element_type=F32) * scale
+        seen = jnp.broadcast_to((mask[r] > 0)[None], (heads, nodes, nodes)).reshape(heads * nodes, nodes)
+        score_new = jnp.where(seen, score_new, -jnp.inf)
+        top = jnp.maximum(jnp.max(score_old, axis=-1, keepdims=True), jnp.max(score_new, axis=-1, keepdims=True))
+        prob_old = jnp.exp(score_old - top)
+        prob_new = jnp.exp(score_new - top)
+        total = jnp.sum(prob_old, axis=-1, keepdims=True) + jnp.sum(prob_new, axis=-1, keepdims=True)
+        mixed = jnp.dot(prob_old.astype(BF16), v_old[r], preferred_element_type=F32)
+        mixed = mixed + jnp.dot(prob_new.astype(BF16), v_new, preferred_element_type=F32)
+        mixed = (mixed / total).astype(BF16)
+        att[pl.ds(r * nodes, nodes), :] = jnp.concatenate([mixed[h * nodes:(h + 1) * nodes] for h in range(heads)], axis=-1)
+
+        shift = length % size
+        window = jnp.concatenate([fresh.astype(F32), jnp.zeros((size, lanes), F32)], axis=0)
+        window = pltpu.roll(window, shift, 0)
+        for j in range(nodes // size + 1):
+            page = table[b * pages + jnp.minimum(length // size + j, pages - 1)]
+            place = row + j * size
+            fits = (place >= shift) & (place < shift + nodes)
+            rows = window[j * size:(j + 1) * size]
+            k_out[page] = jnp.where(fits, rows[:, :dim], k_out[page].astype(F32)).astype(BF16)
+            v_out[page] = jnp.where(fits, rows[:, dim:], v_out[page].astype(F32)).astype(BF16)
+
+
+def attention(hidden, tree_mask, depth, ctx_len, block_table, k_cache, v_cache, attn_norm, w_q, w_k, w_v):
+    requests, nodes, model = hidden.shape
+    blocks, size, kv_local, dim = k_cache.shape
+    pages = block_table.shape[1]
+    per = PER_STEP
+    rows = per * nodes
+    heads = w_q.shape[1] // dim
+    half = dim // 2
+    inv_freq = 1.0 / (ROPE_THETA ** (jnp.arange(half, dtype=F32) * (2.0 / dim)))
+    angles = (ctx_len[:, None] + depth).astype(F32).reshape(requests * nodes, 1) * jnp.tile(inv_freq, 4)[None, :]
+    cosine = jnp.cos(angles)
+    sine = jnp.sin(angles) * jnp.tile(jnp.repeat(jnp.array([-1.0, 1.0], F32), half), 2)[None, :]
+    whole = lambda *shape: pl.BlockSpec(shape, lambda i, *_: (0,) * len(shape))
+    by_row = lambda width: pl.BlockSpec((rows, width), lambda i, *_: (i, 0))
+    cache_type = jax.ShapeDtypeStruct((blocks, size, dim), BF16)
+    att, k_out, v_out = pl.pallas_call(
+        functools.partial(attention_body, per, pages),
+        out_shape=[jax.ShapeDtypeStruct((requests * nodes, heads * dim), BF16), cache_type, cache_type],
+        grid_spec=pltpu.PrefetchScalarGridSpec(
+            num_scalar_prefetch=2,
+            grid=(requests // per,),
+            in_specs=[by_row(model), whole(1, model), whole(model, heads * dim), whole(dim, model), whole(dim, model),
+                      by_row(2 * dim), by_row(2 * dim), pl.BlockSpec((per, nodes, nodes), lambda i, *_: (i, 0, 0)),
+                      whole(blocks, size, dim), whole(blocks, size, dim)],
+            out_specs=[by_row(heads * dim), whole(blocks, size, dim), whole(blocks, size, dim)],
+            scratch_shapes=[pltpu.VMEM((2 * dim, model), BF16), pltpu.VMEM((heads, rows, dim), BF16),
+                            pltpu.VMEM((per, pages * size, dim), BF16), pltpu.VMEM((per, pages * size, dim), BF16)],
+        ),
+        compiler_params=pltpu.CompilerParams(vmem_limit_bytes=48 * 1024 * 1024),
+        cost_estimate=pl.CostEstimate(flops=2 * requests * nodes * model * (heads + 2) * dim, bytes_accessed=hidden.size * 2, transcendentals=0),
+        name="tree_attention",
+    )(ctx_len, block_table.reshape(-1), hidden.reshape(requests * nodes, model), attn_norm.reshape(1, -1), w_q, w_k.T, w_v.T,
+      cosine, sine, tree_mask, k_cache.reshape(blocks, size, dim), v_cache.reshape(blocks, size, dim))
+    return att, k_out.reshape(k_cache.shape), v_out.reshape(v_cache.shape)
 
 
 class Copies:
@@ -127,15 +201,13 @@
         pair[-1].start()
 
     full, rest = vocab // TILE, vocab % TILE
-    count = full + (1 if rest else 0)
+    count = full + 1
+    assert full % 2 == 1 and rest % STEP == 0 and rest > 0
 
     def tile_copy(p, i, size):
         slot = (p * count + i) % 3
         start = i * TILE if isinstance(i, int) else pl.multiple_of(i * TILE, TILE)
         return pltpu.make_async_copy(lm_hbm.at[pl.ds(start, size)], tiles.at[slot, pl.ds(0, size)], s_tile.at[slot])
-
-    def size_of(i):
-        return TILE if i < full else rest
 
     tile_copy(0, 0, TILE).start()
     tile_copy(0, 1, TILE).start()
@@ -243,7 +315,7 @@
         fin[p, pl.ds(pl.multiple_of(core * quad + x * rows, rows), rows), :] = rms_norm(res, gain_f[...])
         ag_start(1, p)
 
-    def mlp(p):
+    def mlp(p, between=None):
         ffn = wg.shape[-1]
         for s in range(2):
             @pl.loop(0, ffn // COLS)
@@ -252,6 +324,9 @@
                 gate = jnp.dot(gat[p], wg[s, :, cols], preferred_element_type=F32)
                 upper = jnp.dot(gat[p], wu[s, :, cols], preferred_element_type=F32)
                 act[s, :, cols] = (jax.nn.silu(gate) * upper).astype(BF16)
+
+            if s == 0 and between is not None:
+                between()
 
         @pl.loop(0, model // COLS)
         def _(n):
@@ -284,6 +359,15 @@
         run[1] = total
         run[2] = chosen
 
+    def prefetch(p, i):
+        @pl.when(i < full)
+        def _():
+            tile_copy(p, i, TILE).start()
+
+        @pl.when(i == full)
+        def _():
+            tile_copy(p, full, rest).start()
+
     def head(p, events):
         run[0] = jnp.full(run.shape[1:], -jnp.inf, F32)
         run[1] = jnp.zeros(run.shape[1:], F32)
@@ -291,41 +375,24 @@
         tile_copy(p, 2, TILE).start()
         multiply(p, 0, TILE, lga)
 
-        def pairs(lo, hi):
-            if lo >= hi:
-                return
-
-            @pl.loop(lo, hi)
-            def _(j):
-                i = 2 * j
-                tile_copy(p, i + 3, TILE).start()
-                multiply(p, i + 1, TILE, lgb)
-                fold(p, i, TILE, lga)
-                tile_copy(p, i + 4, TILE).start()
-                multiply(p, i + 2, TILE, lga)
-                fold(p, i + 1, TILE, lgb)
-
-        loops = (full - 4) // 2
-        cuts = sorted(set([0, loops] + [min(e[0], loops) for e in events]))
-        for e in events:
-            if e[0] == 0:
-                e[1]()
-        for lo, hi in zip(cuts[:-1], cuts[1:]):
-            pairs(lo, hi)
-            for e in events:
-                if min(e[0], loops) == hi and e[0] > 0:
-                    e[1]()
-        done = 2 * loops
-        bufs = (lga, lgb)
-        for i in range(done, count):
-            nxt = i + 3
-            if nxt < count:
-                tile_copy(p, nxt, size_of(nxt)).start()
-            elif p + 1 < chunks and nxt - count < 2:
-                tile_copy(p + 1, nxt - count, TILE).start()
-            if i + 1 < count:
-                multiply(p, i + 1, size_of(i + 1), bufs[(i + 1) % 2])
-            fold(p, i, size_of(i), bufs[i % 2])
+        @pl.loop(0, full // 2)
+        def _(j):
+            for when, event in events:
+                pl.when(j == when)(event)
+            i = 2 * j
+            prefetch(p, i + 3)
+            multiply(p, i + 1, TILE, lgb)
+            fold(p, i, TILE, lga)
+            prefetch(p, i + 4)
+            multiply(p, i + 2, TILE, lga)
+            fold(p, i + 1, TILE, lgb)
+
+        if p + 1 < chunks:
+            tile_copy(p + 1, 0, TILE).start()
+            tile_copy(p + 1, 1, TILE).start()
+        multiply(p, full, rest, lgb)
+        fold(p, full - 1, TILE, lga)
+        fold(p, full, rest, lgb)
         top = jnp.max(run[0], axis=0, keepdims=True)
         total = jnp.sum(run[1] * jnp.exp(run[0] - top), axis=0, keepdims=True)
         chosen = jnp.sum(run[2], axis=0, keepdims=True)
@@ -341,31 +408,34 @@
     for k in range(chunks):
         pair[k].wait_recv()
     pair[chunks].wait_recv()
-    for p in range(chunks):
-        project(p)
-        rs_start(0, p)
+    project(0)
+    rs_start(0, 0)
     wait_loads(chunks + 1, 2 * chunks + 1)
-    for p in range(chunks):
-        rs_merge(0, p)
+    project(1)
+    rs_merge(0, 0)
     attn_end(0)
-    attn_end(1)
     ag_forward(0, 0)
-    ag_forward(0, 1)
+    rs_start(0, 1)
     wait_loads(2 * chunks + 1, len(loads))
     for k in (1, 2, 3):
         pair[chunks + k].wait_recv()
-    for p in range(chunks):
-        ag_wait(0, p)
-        mlp(p)
-        rs_start(1, p)
+    ag_wait(0, 0)
+    mlp(0, lambda: rs_merge(0, 1))
+    rs_start(1, 0)
     rs_merge(1, 0)
     mlp_end(0)
-    rs_merge(1, 1)
-    mlp_end(1)
     ag_forward(1, 0)
+    attn_end(1)
     ag_wait(1, 0)
     dd_wait(0)
-    head(0, [(2, lambda: ag_forward(1, 1)), (6, lambda: ag_wait(1, 1))])
+
+    def second_mlp():
+        ag_wait(0, 1)
+        mlp(1)
+        rs_start(1, 1)
+
+    head(0, [(1, lambda: ag_forward(0, 1)), (3, second_mlp), (5, lambda: rs_merge(1, 1)), (7, lambda: mlp_end(1)),
+             (9, lambda: ag_forward(1, 1)), (11, lambda: ag_wait(1, 1))])
     dd_wait(1)
     head(1, [])
 
@@ -440,23 +510,9 @@
 
     def group_step(hidden, tree_mask, depth, ctx_len, block_table, score_id, k_cache, v_cache, attn_norm, w_q, w_k, w_v, w_o, mlp_norm, w_gate, w_up, w_down, final_norm, w_lm):
         requests, nodes, model = hidden.shape
-        page_size, kv_local, head_dim = k_cache.shape[1:]
-        span = block_table.shape[1] * page_size
-        heads_local = w_q.shape[1] // head_dim
-        normed = rms_norm(hidden, attn_norm)
-        positions = ctx_len[:, None] + depth
-        query = jnp.dot(normed, w_q, preferred_element_type=F32).reshape(requests, nodes, heads_local, head_dim)
-        query = rotate(query, positions).astype(BF16).reshape(requests, nodes, kv_local, heads_local // kv_local, head_dim)
-        key_new = jnp.dot(normed, w_k, preferred_element_type=F32).reshape(requests, nodes, kv_local, head_dim)
-        key_new = rotate(key_new, positions).astype(BF16)
-        val_new = jnp.dot(normed, w_v, preferred_element_type=F32).astype(BF16).reshape(requests, nodes, kv_local, head_dim)
-        key_old = k_cache[block_table].reshape(requests, span, kv_local, head_dim)
-        val_old = v_cache[block_table].reshape(requests, span, kv_local, head_dim)
-        attended = tree_attention(query, key_new, val_new, key_old, val_old, tree_mask, ctx_len)
-        attended = attended.reshape(requests * nodes, heads_local * head_dim)
+        attended, k_out, v_out = attention(hidden, tree_mask, depth, ctx_len, block_table, k_cache, v_cache, attn_norm, w_q, w_k, w_v)
         log_norm, log_prob = tail(tp, attended, hidden.reshape(requests * nodes, model), w_o, w_gate, w_up, w_down, w_lm, mlp_norm, final_norm, score_id)
-        return (log_norm.reshape(requests, nodes), log_prob.reshape(requests, nodes),
-                write_cache(k_cache, block_table, ctx_len, key_new), write_cache(v_cache, block_table, ctx_len, val_new))
+        return log_norm.reshape(requests, nodes), log_prob.reshape(requests, nodes), k_out, v_out
 
     request_spec = P("dp", None, None)
     node_spec = P("dp", None)

time: 275 us -> 222 us (0.81); the launches traced: 271 us -> 222 us
  local copies, waits for them, and re-layouts: 41.7 us -> 18.8 us
  matrix products: 17.1 us -> 0 us
  other arithmetic: 16.1 us -> 2.82 us
  Pallas kernels: 194 us -> 200 us
    pallas_call x0 -> x1, Pallas kernels: none -> 21.7 us  [attention(): pl.pallas_call(functools.partial(attention_body, per, pages), out_shape=[...]
    dot_general x7 -> x0, matrix products: 17.1 us -> none  [the longest x1 4.54 us: tree_attention(): jnp.einsum('btkgs,bskh->btkgh', prob_old.astype(BF16), val_old, preferred...]
    pallas_call x1, Pallas kernels: 194 us -> 178 us  [tail(): pl.pallas_call(functools.partial(tail_body, tp), out_shape=[jax.ShapeDtyp...]
    gather x5 -> x0, local copies, waits for them, and re-layouts: 11.8 us -> none  [the longest x3 7.35 us: write_cache(): slot_blocks = jnp.take_along_axis(table, slots // page_size, axis=1)]
    reduce_sum x3 -> x0, other arithmetic: 5.69 us -> none  [the longest x1 3.23 us: rms_norm(): jnp.mean(widened * widened, axis=-1, keepdims=True) + RMS_EPS]
    unnamed x59 -> x28, local copies, waits for them, and re-layouts: 18.5 us -> 13.1 us
    another operation x2 -> x0, other arithmetic: 4.36 us -> none
    slice x1 -> x0, local copies, waits for them, and re-layouts: 3.26 us -> none  [rotate(): first = values[..., :half]]
where the time goes in v2:
time: 222 us
  Pallas kernels  200 us (90%)
  local copies, waits for them, and re-layouts  18.8 us (8%)
  other arithmetic  2.82 us (1%)
    pallas_call x1, Pallas kernels, tail(): pl.pallas_call(functools.partial(tail_body, tp), out_shape=[jax.ShapeDtyp...  178 us
    pallas_call x1, Pallas kernels, attention(): pl.pallas_call(functools.partial(attention_body, per, pages), out_shape=[...  21.7 us
    unnamed x28, local copies, waits for them, and re-layouts  13.1 us

profile of v2, /device:TPU:81, one launch (start us, length us, event | category | flops | bytes accessed | tf_op | source)
XLA Modules:
  0.0 222.0 jit_solution(2114976968634117260)
XLA Ops:
  0.6 0.0 copy-start.5
  0.6 0.0 copy-start.9
  0.7 0.0 copy-start.7
  0.7 0.0 copy-start.3
  0.7 0.0 copy-start.4
  0.7 0.0 copy-start.2
  0.7 0.0 copy-start.1
  0.7 0.9 add_convert_fusion
  1.6 0.1 mul.37
  1.7 0.1 mul.41
  1.8 0.7 broadcast_in_dim.11
  2.5 0.1 tile.14
  2.6 0.1 mul.44
  2.7 1.9 fusion
  4.6 2.8 %copy.24 = bf16[384,16,1,64]{3,1,0,2:T(8,128)(2,1)} copy(bf16[384,16,1,64]{0,3,2,1:T(8,128)(2,1)} %param.26) | data formatting | bytes 1572864 | tf_op args[6]
  7.4 2.9 %copy.25 = bf16[384,16,1,64]{3,1,0,2:T(8,128)(2,1)} copy(bf16[384,16,1,64]{0,3,2,1:T(8,128)(2,1)} %param.27) | data formatting | bytes 1572864 | tf_op args[7]
  10.3 0.0 copy-done.9
  10.3 0.0 copy-done.7
  10.3 0.1 reshape.56.table
  10.4 0.0 copy-done.5
  10.4 0.0 copy-done.3
  10.4 0.0 copy-done.4
  10.4 0.0 copy-done.2
  10.4 0.0 copy-done.1
  10.4 0.0 copy-start.8
  10.4 0.0 copy-start.10
  10.5 0.0 copy-start.11
  10.5 21.7 %tree_attention.1 = (bf16[1024,256]{1,0:T(8,128)(2,1)S(1)}, bf16[384,16,64]{2,1,0:T(8,128)(2,1)S(1)}, bf16[384,16,64]{2,1,0:T(8,128)(2,1)}) custom-call(s32[16]{0:T(128)S(1)} %copy-done.5, s32[384]{0:T(512)S(1)} %reshape.56.table, bf16[1024,2048]{1,0:T(8,128)(2,1)} %bitcast.13, bf16[1,2048]{1,0:T(2,128)(2,1)S(1)} %reshape.58.gain, ...), custom_call_target="tpu_custom_call" | custom-call | flops 1610612736 | bytes 4194304 | tf_op jit(solution)/shard_map/tree_attention/pallas_call | solution.py:117
  32.1 0.0 copy-start
  32.1 1.1 copy-done
  33.3 0.0 copy-start.6
  33.3 0.8 copy-done.6
  34.1 0.0 copy-done.8
  34.1 0.1 broadcast_in_dim.12
  34.1 0.6 broadcast_in_dim.13.target
  34.8 0.0 copy-done.10
  34.8 0.6 reshape.61.gain_m
  35.4 0.0 copy-done.11
  35.4 0.6 reshape.62.gain_f
  36.0 177.9 %layer_tail_and_head.1 = (f32[8,128]{1,0:T(8,128)}, f32[8,128]{1,0:T(8,128)}) custom-call(bf16[1024,256]{1,0:T(8,128)(2,1)} %copy-done.6, bf16[1024,2048]{1,0:T(8,128)(2,1)} %bitcast.14, bf16[256,2048]{1,0:T(8,128)(2,1)} %wo_hbm.1, bf16[2048,1024]{1,0:T(8,128)(2,1)} %wg_hbm.1, bf16[2048,1024]{1,0:T(8,128)(2,1)} %wu_hbm.1, bf16[1024,2048]{1,0:T(8,128)(2,1)} %wd_hbm.1, ...), custom_call_target="tpu_custom_call" | custom-call | flops 81201725440 | bytes 131334144 | tf_op jit(solution)/shard_map/layer_tail_and_head/pallas_call | solution.py:482
  213.9 1.3 reshape.63
  215.3 1.3 reshape.64
  216.6 2.7 %copy.26 = bf16[384,16,1,64]{0,3,2,1:T(8,128)(2,1)} copy(bf16[384,16,1,64]{3,1,0,2:T(8,128)(2,1)} %bitcast.8) | data formatting | bytes 1572864
  219.3 2.7 %copy.27 = bf16[384,16,1,64]{0,3,2,1:T(8,128)(2,1)} copy(bf16[384,16,1,64]{3,1,0,2:T(8,128)(2,1)} %bitcast.15) | data formatting | bytes 1572864
  (4 shorter events, 0.0 us)
Async XLA Ops:
  0.6 9.8 %copy-start.5 = (s32[16]{0:T(128)S(1)}, s32[16]{0:T(128)}, u32[]{:S(2)}) copy-start(s32[16]{0:T(128)} %ctx.1) | copy-start | bytes 196
  0.6 9.6 %copy-start.9 = (bf16[2048]{0:T(1024)(128)(2,1)S(1)}, bf16[2048]{0:T(1024)(128)(2,1)}, u32[]{:S(2)}) copy-start(bf16[2048]{0:T(1024)(128)(2,1)} %param.28) | copy-start | bytes 12292
  0.7 9.6 %copy-start.7 = (s32[16,24]{1,0:T(8,128)S(1)}, s32[16,24]{1,0:T(8,128)}, u32[]{:S(2)}) copy-start(s32[16,24]{1,0:T(8,128)} %param.24) | copy-start | bytes 4612
  0.7 9.7 %copy-start.3 = (bf16[2048,64]{0,1:T(8,128)(2,1)S(1)}, bf16[2048,64]{0,1:T(8,128)(2,1)}, u32[]{:S(2)}) copy-start(bf16[2048,64]{0,1:T(8,128)(2,1)} %param.30) | copy-start | bytes 786436
  0.7 9.7 %copy-start.4 = (bf16[2048,64]{0,1:T(8,128)(2,1)S(1)}, bf16[2048,64]{0,1:T(8,128)(2,1)}, u32[]{:S(2)}) copy-start(bf16[2048,64]{0,1:T(8,128)(2,1)} %param.31) | copy-start | bytes 786436
  0.7 9.7 %copy-start.2 = (s32[16,64,64]{2,1,0:T(8,128)S(1)}, s32[16,64,64]{2,1,0:T(8,128)}, u32[]{:S(2)}) copy-start(s32[16,64,64]{2,1,0:T(8,128)} %mask.1) | copy-start | bytes 786436
  0.7 9.7 %copy-start.1 = (bf16[2048,256]{1,0:T(8,128)(2,1)S(1)}, bf16[2048,256]{1,0:T(8,128)(2,1)}, u32[]{:S(2)}) copy-start(bf16[2048,256]{1,0:T(8,128)(2,1)} %w_q.1) | copy-start | bytes 3145732
  10.4 23.6 %copy-start.8 = (s32[16,64]{1,0:T(8,128)S(1)}, s32[16,64]{1,0:T(8,128)}, u32[]{:S(2)}) copy-start(s32[16,64]{1,0:T(8,128)} %param.25) | copy-start | bytes 12292
  10.4 24.3 %copy-start.10 = (bf16[2048]{0:T(1024)(128)(2,1)S(1)}, bf16[2048]{0:T(1024)(128)(2,1)}, u32[]{:S(2)}) copy-start(bf16[2048]{0:T(1024)(128)(2,1)} %param.33) | copy-start | bytes 12292
  10.5 24.9 %copy-start.11 = (bf16[2048]{0:T(1024)(128)(2,1)S(1)}, bf16[2048]{0:T(1024)(128)(2,1)}, u32[]{:S(2)}) copy-start(bf16[2048]{0:T(1024)(128)(2,1)} %param.37) | copy-start | bytes 12292
  32.1 1.1 copy-start
  33.3 0.8 copy-start.6

commit v3 on v2

v3 whole, which is shorter than its diff:
```python
import functools

import jax
import jax.numpy as jnp
from jax import lax
from jax.experimental import pallas as pl
from jax.experimental.pallas import tpu as pltpu
from jax.sharding import PartitionSpec as P

RMS_EPS = 1e-5
ROPE_THETA = 500000
CHIPS = 4
PER_STEP = 4
SHARES = (1, 1, 2)
TILE = 1024
COLS = 512
STEP = 32
VMEM_LIMIT = 67043328
F32 = jnp.float32
BF16 = jnp.bfloat16


def rms_norm(values, gain):
    widened = values.astype(F32)
    scale = lax.rsqrt(jnp.mean(widened * widened, axis=-1, keepdims=True) + RMS_EPS)
    return (widened * scale * gain.astype(F32)).astype(BF16)


def attention_body(per, pages, ctx, table, hidden, gain, w_q, w_k, w_v, cosine, sine, mask, k_in, v_in, att, k_out, v_out, w_kv, q_heads, kv_old, kv):
    step = pl.program_id(0)
    nodes = mask.shape[1]
    size, dim, blocks = k_in.shape
    lanes = 2 * dim
    pitch = kv.shape[0] // size
    heads = w_q.shape[1] // dim
    span = pages * size

    @pl.when(step == 0)
    def _():
        w_kv[pl.ds(0, dim), :] = w_k[...]
        w_kv[pl.ds(dim, dim), :] = w_v[...]
        for s in range(size):
            joined = jnp.concatenate([k_in[s].astype(F32), v_in[s].astype(F32)], axis=0)
            kv[pl.ds(s * pitch, blocks), :] = joined.T

    normed = rms_norm(hidden[...], gain[...].reshape(1, -1))
    nt = (((1,), (1,)), ((), ()))
    queries = jnp.dot(normed, w_q[...], preferred_element_type=F32)
    pair = lax.dot_general(normed, w_kv[...], nt, preferred_element_type=F32)
    lane = lax.broadcasted_iota(jnp.int32, (per * nodes, lanes), 1)
    lower = (lane % dim) < dim // 2

    def rotate(values):
        swapped = jnp.where(lower, pltpu.roll(values, lanes - dim // 2, 1), pltpu.roll(values, dim // 2, 1))
        return values * cosine[...] + swapped * sine[...]

    for h in range(0, heads, 2):
        turned = rotate(queries[:, h * dim:(h + 2) * dim])
        q_heads[h] = jnp.where(lane < dim, turned, 0.0).astype(BF16)
        q_heads[h + 1] = jnp.where(lane < dim, pltpu.roll(turned, dim, 1), 0.0).astype(BF16)
    pair = jnp.where(lane < dim, rotate(pair), pair).astype(BF16)
    scale = dim ** -0.5
    slot = lax.broadcasted_iota(jnp.int32, (heads * nodes, span), 1)
    row = lax.broadcasted_iota(jnp.int32, (size, lanes), 0)
    for r in range(per):
        b = step * per + r
        length = ctx[b]
        for j in range(pages):
            kv_old[r, pl.ds(j * size, size), :] = kv[pl.ds(table[b, j], size, stride=pitch), :].astype(BF16)
        fresh = pair[r * nodes:(r + 1) * nodes]
        query = q_heads[:, pl.ds(r * nodes, nodes), :].reshape(heads * nodes, lanes)
        score_old = lax.dot_general(query, kv_old[r], nt, preferred_element_type=F32) * scale
        score_old = jnp.where(slot < length, score_old, -jnp.inf)
        score_new = lax.dot_general(query, fresh, nt, preferred_element_type=F32) * scale
        seen = jnp.broadcast_to((mask[r] > 0)[None], (heads, nodes, nodes)).reshape(heads * nodes, nodes)
        score_new = jnp.where(seen, score_new, -jnp.inf)
        top = jnp.maximum(jnp.max(score_old, axis=-1, keepdims=True), jnp.max(score_new, axis=-1, keepdims=True))
        prob_old = jnp.exp(score_old - top)
        prob_new = jnp.exp(score_new - top)
        total = jnp.sum(prob_old, axis=-1, keepdims=True) + jnp.sum(prob_new, axis=-1, keepdims=True)
        mixed = jnp.dot(prob_old.astype(BF16), kv_old[r], preferred_element_type=F32)
        mixed = mixed + jnp.dot(prob_new.astype(BF16), fresh, preferred_element_type=F32)
        mixed = mixed / total
        for h in range(0, heads, 2):
            even = pltpu.roll(mixed[h * nodes:(h + 1) * nodes], dim, 1)
            odd = mixed[(h + 1) * nodes:(h + 2) * nodes]
            joined = jnp.where(lane[:nodes] < dim, even, odd)
            att[pl.ds(r * nodes, nodes), h * dim:(h + 2) * dim] = joined.astype(BF16)

        shift = length % size
        window = jnp.concatenate([fresh.astype(F32), jnp.zeros((size, lanes), F32)], axis=0)
        window = pltpu.roll(window, shift, 0)
        for j in range(nodes // size + 1):
            page = table[b, jnp.minimum(length // size + j, pages - 1)]
            place = row + j * size
            fits = (place >= shift) & (place < shift + nodes)
            at = pl.ds(page, size, stride=pitch)
            kv[at, :] = jnp.where(fits, window[j * size:(j + 1) * size], kv[at, :])

    @pl.when(step == pl.num_programs(0) - 1)
    def _():
        for s in range(size):
            apart = kv[pl.ds(s * pitch, blocks), :].T.astype(BF16)
            k_out[s] = apart[:dim]
            v_out[s] = apart[dim:]


def attention(hidden, tree_mask, depth, ctx_len, block_table, k_cache, v_cache, attn_norm, w_q, w_k, w_v):
    requests, nodes, model = hidden.shape
    blocks, size, kv_local, dim = k_cache.shape
    pages = block_table.shape[1]
    per = PER_STEP
    rows = per * nodes
    heads = w_q.shape[1] // dim
    half = dim // 2
    lane = jnp.arange(2 * dim)
    inv_freq = 1.0 / (ROPE_THETA ** ((lane % half).astype(F32) * (2.0 / dim)))
    angles = (ctx_len[:, None] + depth).astype(F32)[..., None] * inv_freq
    cosine = jnp.cos(angles).reshape(requests * nodes, 2 * dim)
    sine = (jnp.sin(angles) * jnp.where(lane % dim < half, -1.0, 1.0)).reshape(requests * nodes, 2 * dim)
    stored = lambda cache: cache.transpose(1, 2, 3, 0).reshape(size, dim, blocks)
    native = lambda cache: cache.reshape(size, kv_local, dim, blocks).transpose(3, 0, 1, 2)
    cache_type = jax.ShapeDtypeStruct((size, dim, blocks), BF16)
    whole = lambda *shape: pl.BlockSpec(shape, lambda i, *_: (0,) * len(shape))
    by_row = lambda width: pl.BlockSpec((rows, width), lambda i, *_: (i, 0))
    att, k_out, v_out = pl.pallas_call(
        functools.partial(attention_body, per, pages),
        out_shape=[jax.ShapeDtypeStruct((requests * nodes, heads * dim), BF16), cache_type, cache_type],
        grid_spec=pltpu.PrefetchScalarGridSpec(
            num_scalar_prefetch=2,
            grid=(requests // per,),
            in_specs=[by_row(model), whole(model), whole(model, heads * dim), whole(dim, model), whole(dim, model),
                      by_row(2 * dim), by_row(2 * dim), pl.BlockSpec((per, nodes, nodes), lambda i, *_: (i, 0, 0)),
                      whole(size, dim, blocks), whole(size, dim, blocks)],
            out_specs=[by_row(heads * dim), whole(size, dim, blocks), whole(size, dim, blocks)],
            scratch_shapes=[pltpu.VMEM((2 * dim, model), BF16), pltpu.VMEM((heads, rows, 2 * dim), BF16),
                            pltpu.VMEM((per, pages * size, 2 * dim), BF16), pltpu.VMEM((size * (blocks + 8), 2 * dim), F32)],
        ),
        compiler_params=pltpu.CompilerParams(vmem_limit_bytes=VMEM_LIMIT),
        cost_estimate=pl.CostEstimate(flops=2 * requests * nodes * model * (heads + 2) * dim, bytes_accessed=hidden.size * 2, transcendentals=0),
        name="tree_attention",
    )(ctx_len, block_table, hidden.reshape(requests * nodes, model), attn_norm, w_q, w_k.T, w_v.T,
      cosine, sine, tree_mask, stored(k_cache), stored(v_cache))
    return att, native(k_out), native(v_out)


class Copies:
    def __init__(self, make, plan):
        self.make = make
        self.plan = plan

    def __getitem__(self, k):
        return self.make(*self.plan[k]())

    def all(self):
        return [self[k] for k in range(len(self.plan))]


def tail_body(tp, att_hbm, hid_hbm, wo_hbm, wg_hbm, wu_hbm, wd_hbm, lm_hbm, gain_m, gain_f, target, norm_out, prob_out,
              att_own, att_far, hid, wo, wg, wu, wd, part, mrg_in, mrg_out, fin_in, h1, gat, fin, act, tiles, lga, lgb, run, stats,
              s_load, s_pair_s, s_pair_r, s_rs_s, s_rs_r, s_ag_s, s_ag_r, s_dd_s, s_dd_r, s_tile, s_st_s, s_st_r):
    me = lax.axis_index("tp")
    x = me // 2
    core = me % 2
    right = 2 * ((x + 1) % CHIPS) + core
    left = 2 * ((x + CHIPS - 1) % CHIPS) + core
    partner = me + 1 - 2 * core
    chunks = len(SHARES)
    rows = [h1.shape[0] * share // sum(SHARES) for share in SHARES]
    base = [sum(rows[:p]) for p in range(chunks)]
    vocab = lm_hbm.shape[0]
    model = hid.shape[-1]

    def own(p):
        return pl.ds(base[p], rows[p])

    def quad(p):
        return pl.ds(CHIPS * base[p], CHIPS * rows[p])

    def wide(p):
        return pl.ds(2 * CHIPS * base[p], 2 * CHIPS * rows[p])

    def front(p):
        return pl.ds(base[p] // 2, rows[p] // 2)

    def block(p, b, lo, n):
        return pl.ds(pl.multiple_of(CHIPS * base[p] + (b % CHIPS) * rows[p] + lo, rows[p] // 2), n)

    def placed(p, b, lo, n):
        return pl.ds(pl.multiple_of(CHIPS * (2 * base[p] + core * rows[p]) + (b % CHIPS) * rows[p] + lo, rows[p] // 2), n)

    def remote(src, dst, ssem, rsem, dev):
        return pltpu.make_async_remote_copy(src_ref=src, dst_ref=dst, send_sem=ssem, recv_sem=rsem,
                                            device_id={"tp": dev}, device_id_type=pl.DeviceIdType.MESH)

    barrier = pltpu.get_barrier_semaphore()
    for k in range(1, tp):
        pl.semaphore_signal(barrier, inc=1, device_id={"tp": (me + k) % tp}, device_id_type=pl.DeviceIdType.MESH)

    def token_rows(p, c):
        return pl.ds(pl.multiple_of(CHIPS * (2 * base[p] + c * rows[p]), CHIPS * rows[p]), CHIPS * rows[p])

    loads = []

    def load(src, dst):
        loads.append(pltpu.make_async_copy(src, dst, s_load.at[len(loads)]))
        loads[-1].start()

    for p in range(chunks):
        load(att_hbm.at[token_rows(p, core)], att_own.at[quad(p)])
    load(wo_hbm, wo.at[0])
    for p in range(chunks):
        load(hid_hbm.at[placed(p, x, 0, rows[p])], hid.at[own(p)])
    load(wg_hbm, wg.at[0])
    load(wu_hbm, wu.at[0])
    load(wd_hbm, wd.at[0])

    pl.semaphore_wait(barrier, tp - 1)

    pair = []
    for src, dst in ([(att_hbm.at[token_rows(p, 1 - core)], att_far.at[quad(p)]) for p in range(chunks)] +
                     [(wo_hbm, wo.at[1]), (wg_hbm, wg.at[1]), (wu_hbm, wu.at[1]), (wd_hbm, wd.at[1])]):
        pair.append(remote(src, dst, s_pair_s.at[len(pair)], s_pair_r.at[len(pair)], partner))
        pair[-1].start()

    full, rest = vocab // TILE, vocab % TILE
    count = full + 1
    assert full % 2 == 1 and rest % STEP == 0 and rest > 0

    def tile_copy(p, i, size):
        slot = (p * count + i) % 3
        start = i * TILE if isinstance(i, int) else pl.multiple_of(i * TILE, TILE)
        return pltpu.make_async_copy(lm_hbm.at[pl.ds(start, size)], tiles.at[slot, pl.ds(0, size)], s_tile.at[slot])

    tile_copy(0, 0, TILE).start()
    tile_copy(0, 1, TILE).start()

    def project(p):
        @pl.loop(0, model // COLS)
        def _(n):
            cols = pl.ds(pl.multiple_of(n * COLS, COLS), COLS)
            acc = jnp.dot(att_own[quad(p), :], wo[0, :, cols], preferred_element_type=F32)
            acc = acc + jnp.dot(att_far[quad(p), :], wo[1, :, cols], preferred_element_type=F32)
            part[0, quad(p), cols] = acc.astype(BF16)

    def rs_copies(ph, p):
        mine = part.at[ph]
        half = rows[p] // 2
        sem = lambda k: (s_rs_s.at[ph, p, k], s_rs_r.at[ph, p, k])
        top, low = pl.ds(base[p], half), pl.ds(base[p] + half, half)
        plan = [
            lambda: (mine.at[block(p, x + 2, 0, half)], mrg_in.at[ph, 0, front(p)], *sem(0), right),
            lambda: (mine.at[block(p, x + 2, half, half)], mrg_in.at[ph, 1, front(p)], *sem(1), left),
            lambda: (mine.at[block(p, x + 1, half, half)], fin_in.at[ph, 0, low], *sem(2), right),
            lambda: (mine.at[block(p, x + 3, 0, half)], fin_in.at[ph, 1, top], *sem(3), left),
            lambda: (mrg_out.at[ph, 0, front(p)], fin_in.at[ph, 0, top], *sem(4), right),
            lambda: (mrg_out.at[ph, 1, front(p)], fin_in.at[ph, 1, low], *sem(5), left),
        ]
        return Copies(remote, plan)

    def rs_start(ph, p):
        for k in range(4):
            rs_copies(ph, p)[k].start()

    def rs_merge(ph, p):
        c = rs_copies(ph, p)
        half = rows[p] // 2
        c[0].wait_recv()
        mrg_out[ph, 0, front(p), :] = (part[ph, block(p, x + 1, 0, half), :].astype(F32) + mrg_in[ph, 0, front(p), :].astype(F32)).astype(BF16)
        c[4].start()
        c[1].wait_recv()
        mrg_out[ph, 1, front(p), :] = (part[ph, block(p, x + 3, half, half), :].astype(F32) + mrg_in[ph, 1, front(p), :].astype(F32)).astype(BF16)
        c[5].start()

    def rs_finish(ph, p):
        c = rs_copies(ph, p)
        for k in (2, 3, 4, 5):
            c[k].wait_recv()
        total = part[ph, block(p, x, 0, rows[p]), :].astype(F32) + fin_in[ph, 0, own(p), :].astype(F32) + fin_in[ph, 1, own(p), :].astype(F32)
        return total.astype(BF16).astype(F32)

    def ag_copies(ph, p):
        half = rows[p] // 2
        if ph == 0:
            at = lambda b, lo: gat.at[block(p, b, lo, half)]
        else:
            at = lambda b, lo: fin.at[placed(p, b, lo, half)]
        sem = lambda k: (s_ag_s.at[ph, p, k], s_ag_r.at[ph, p, k])
        plan = [(x, 0, right), (x, half, right), (x, half, left), (x, 0, left), (x + 3, 0, right), (x + 1, half, left)]
        return Copies(remote, [lambda k=k, b=b, lo=lo, dev=dev: (at(b, lo), at(b, lo), *sem(k), dev) for k, (b, lo, dev) in enumerate(plan)])

    def dd_copies(p):
        def plan(k):
            at = fin.at[placed(p, x + k, 0, rows[p])]
            return at, at, s_dd_s.at[p, k], s_dd_r.at[p, k], partner

        return Copies(remote, [functools.partial(plan, k) for k in range(CHIPS)])

    def ag_start(ph, p):
        c = ag_copies(ph, p)
        for k in (0, 2, 1, 3):
            c[k].start()
        if ph == 1:
            dd_copies(p)[0].start()

    def ag_forward(ph, p):
        c = ag_copies(ph, p)
        c[0].wait_recv()
        c[4].start()
        c[2].wait_recv()
        c[5].start()

    def ag_wait(ph, p):
        c = ag_copies(ph, p)
        d = dd_copies(p)
        c[1].wait_recv()
        if ph == 1:
            d[3].start()
        c[3].wait_recv()
        if ph == 1:
            d[1].start()
        c[4].wait_recv()
        c[5].wait_recv()
        if ph == 1:
            d[2].start()

    def dd_wait(p):
        for d in dd_copies(p).all():
            d.wait_recv()

    def attn_end(p):
        summed = rs_finish(0, p)
        res = (hid[own(p), :].astype(F32) + summed).astype(BF16)
        h1[own(p), :] = res
        gat[block(p, x, 0, rows[p]), :] = rms_norm(res, gain_m[...].reshape(1, -1))
        ag_start(0, p)

    def mlp_end(p):
        summed = rs_finish(1, p)
        res = (h1[own(p), :].astype(F32) + summed).astype(BF16)
        fin[placed(p, x, 0, rows[p]), :] = rms_norm(res, gain_f[...].reshape(1, -1))
        ag_start(1, p)

    def mlp(p, between=None):
        ffn = wg.shape[-1]
        used = pl.ds(0, CHIPS * rows[p])
        for s in range(2):
            @pl.loop(0, ffn // COLS)
            def _(n):
                cols = pl.ds(pl.multiple_of(n * COLS, COLS), COLS)
                gate = jnp.dot(gat[quad(p), :], wg[s, :, cols], preferred_element_type=F32)
                upper = jnp.dot(gat[quad(p), :], wu[s, :, cols], preferred_element_type=F32)
                act[s, used, cols] = (jax.nn.silu(gate) * upper).astype(BF16)

            if s == 0 and between is not None:
                between()

        @pl.loop(0, model // COLS)
        def _(n):
            cols = pl.ds(pl.multiple_of(n * COLS, COLS), COLS)
            acc = jnp.dot(act[0, used, :], wd[0, :, cols], preferred_element_type=F32)
            acc = acc + jnp.dot(act[1, used, :], wd[1, :, cols], preferred_element_type=F32)
            part[1, quad(p), cols] = acc.astype(BF16)

    def multiply(p, i, size, out):
        slot = (p * count + i) % 3
        tile_copy(p, i, size).wait()
        span = 2 * CHIPS * rows[p]
        cut = size if span > 256 else size // 2
        for r in range(0, size, cut):
            out[pl.ds(r, cut), pl.ds(0, span)] = lax.dot_general(
                tiles[slot, pl.ds(r, cut), :], fin[wide(p), :], (((1,), (1,)), ((), ())), preferred_element_type=F32)

    def fold(p, i, size, src):
        span = 2 * CHIPS * rows[p]
        cols = pl.ds(0, span)
        goal = target[:, wide(p)] - (me * vocab + i * TILE) - lax.broadcasted_iota(jnp.int32, (8, span), 0)
        depth = STEP // 8
        offsets = 8 * lax.broadcasted_iota(jnp.int32, (depth, 8, span), 0)
        old = run[0, :, cols]
        top = old
        for r in range(0, size, STEP):
            top = jnp.maximum(top, jnp.max(src[pl.ds(r, STEP), cols].reshape(depth, 8, span), axis=0))
        total = run[1, :, cols] * jnp.exp(old - top)
        chosen = run[2, :, cols]
        for r in range(0, size, STEP):
            piece = src[pl.ds(r, STEP), cols].reshape(depth, 8, span)
            total = total + jnp.sum(jnp.exp(piece - top[None]), axis=0)
            chosen = chosen + jnp.sum(jnp.where((goal - r)[None] == offsets, piece, 0.0), axis=0)
        run[0, :, cols] = top
        run[1, :, cols] = total
        run[2, :, cols] = chosen

    def prefetch(p, i):
        @pl.when(i < full)
        def _():
            tile_copy(p, i, TILE).start()

        @pl.when(i == full)
        def _():
            tile_copy(p, full, rest).start()

    def head(p, events):
        run[0] = jnp.full(run.shape[1:], -jnp.inf, F32)
        run[1] = jnp.zeros(run.shape[1:], F32)
        run[2] = jnp.zeros(run.shape[1:], F32)
        tile_copy(p, 2, TILE).start()
        multiply(p, 0, TILE, lga)

        @pl.loop(0, full // 2)
        def _(j):
            for when, event in events:
                pl.when(j == when)(event)
            i = 2 * j
            prefetch(p, i + 3)
            multiply(p, i + 1, TILE, lgb)
            fold(p, i, TILE, lga)
            prefetch(p, i + 4)
            multiply(p, i + 2, TILE, lga)
            fold(p, i + 1, TILE, lgb)

        if p + 1 < chunks:
            tile_copy(p + 1, 0, TILE).start()
            tile_copy(p + 1, 1, TILE).start()
        multiply(p, full, rest, lgb)
        fold(p, full - 1, TILE, lga)
        fold(p, full, rest, lgb)
        span = 2 * CHIPS * rows[p]
        cols = pl.ds(0, span)
        top = jnp.max(run[0, :, cols], axis=0, keepdims=True)
        total = jnp.sum(run[1, :, cols] * jnp.exp(run[0, :, cols] - top), axis=0, keepdims=True)
        chosen = jnp.sum(run[2, :, cols], axis=0, keepdims=True)
        for k, row in enumerate((top, total, chosen)):
            for g in range(span // 128):
                stats[me, k, pl.ds(2 * CHIPS * base[p] // 128 + g, 1), :] = row[:, g * 128:(g + 1) * 128]

    def wait_loads(lo, hi):
        for k in range(lo, hi):
            loads[k].wait()

    wait_loads(0, chunks + 1)
    for k in range(chunks):
        pair[k].wait_recv()
    pair[chunks].wait_recv()
    project(0)
    rs_start(0, 0)
    wait_loads(chunks + 1, 2 * chunks + 1)
    project(1)
    project(2)
    rs_merge(0, 0)
    attn_end(0)
    ag_forward(0, 0)
    rs_start(0, 1)
    wait_loads(2 * chunks + 1, len(loads))
    for k in (1, 2, 3):
        pair[chunks + k].wait_recv()
    ag_wait(0, 0)
    mlp(0, lambda: rs_merge(0, 1))
    rs_start(1, 0)
    rs_merge(1, 0)
    mlp_end(0)
    ag_forward(1, 0)
    attn_end(1)
    ag_wait(1, 0)
    dd_wait(0)

    def forward_and_start():
        ag_forward(0, 1)
        rs_start(0, 2)

    def feed(p):
        ag_wait(0, p)
        mlp(p)
        rs_start(1, p)

    def forward_and_end():
        ag_forward(1, 1)
        attn_end(2)

    head(0, [(0, forward_and_start), (1, lambda: feed(1)), (2, lambda: rs_merge(0, 2)), (3, lambda: rs_merge(1, 1)),
             (4, lambda: mlp_end(1)), (5, forward_and_end), (6, lambda: ag_wait(1, 1))])
    dd_wait(1)
    head(1, [(0, lambda: ag_forward(0, 2)), (1, lambda: feed(2)), (3, lambda: rs_merge(1, 2)), (4, lambda: mlp_end(2)),
             (6, lambda: ag_forward(1, 2))])
    ag_wait(1, 2)
    dd_wait(2)
    head(2, [])

    sent = []
    for k in range(1, tp):
        sent.append(remote(stats.at[me], stats.at[me], s_st_s.at[k - 1], s_st_r.at[k - 1], (me + k) % tp))
        sent[-1].start()
    for d in sent:
        d.wait_recv()
    top = stats[0, 0]
    for k in range(1, tp):
        top = jnp.maximum(top, stats[k, 0])
    total = jnp.zeros_like(top)
    chosen = jnp.zeros_like(top)
    for k in range(tp):
        total = total + stats[k, 1] * jnp.exp(stats[k, 0] - top)
        chosen = chosen + stats[k, 2]
    log_norm = top + jnp.log(total)
    norm_out[...] = log_norm
    prob_out[...] = chosen - log_norm

    for d in sent + pair:
        d.wait_send()
    for p in range(chunks):
        for ph in range(2):
            for d in rs_copies(ph, p).all() + ag_copies(ph, p).all():
                d.wait_send()
        for d in dd_copies(p).all():
            d.wait_send()


def tail(tp, attended, hidden, w_o, w_gate, w_up, w_down, w_lm, mlp_norm, final_norm, score_id):
    tokens, model = hidden.shape
    heads = attended.shape[-1]
    ffn = w_gate.shape[-1]
    chunks = len(SHARES)
    rows = tokens // tp
    quad = CHIPS * rows
    most = tokens * max(SHARES) // sum(SHARES)
    target = jnp.broadcast_to(score_id.reshape(1, tokens), (8, tokens))
    anyspace = pl.BlockSpec(memory_space=pl.ANY)
    vmem = pl.BlockSpec(memory_space=pltpu.VMEM)
    dma = pltpu.SemaphoreType.DMA
    flops = 2 * tokens * model * (w_lm.shape[-1] + 3 * ffn + heads)
    log_norm, log_prob = pl.pallas_call(
        functools.partial(tail_body, tp),
        out_shape=[jax.ShapeDtypeStruct((tokens // 128, 128), F32)] * 2,
        in_specs=[anyspace] * 7 + [vmem] * 3,
        out_specs=[vmem] * 2,
        scratch_shapes=[
            pltpu.VMEM((quad, heads), BF16), pltpu.VMEM((quad, heads), BF16),
            pltpu.VMEM((rows, model), BF16), pltpu.VMEM((2, heads, model), BF16),
            pltpu.VMEM((2, model, ffn), BF16), pltpu.VMEM((2, model, ffn), BF16), pltpu.VMEM((2, ffn, model), BF16),
            pltpu.VMEM((2, quad, model), BF16), pltpu.VMEM((2, 2, rows // 2, model), BF16),
            pltpu.VMEM((2, 2, rows // 2, model), BF16), pltpu.VMEM((2, 2, rows, model), BF16),
            pltpu.VMEM((rows, model), BF16), pltpu.VMEM((quad, model), BF16),
            pltpu.VMEM((tokens, model), BF16), pltpu.VMEM((2, most // 2, ffn), BF16),
            pltpu.VMEM((3, TILE, model), BF16), pltpu.VMEM((TILE, most), F32), pltpu.VMEM((TILE, most), F32),
            pltpu.VMEM((3, 8, most), F32), pltpu.VMEM((tp, 3, tokens // 128, 128), F32),
            dma((2 * chunks + 4,)), dma((chunks + 4,)), dma((chunks + 4,)),
            dma((2, chunks, 6)), dma((2, chunks, 6)), dma((2, chunks, 6)), dma((2, chunks, 6)),
            dma((chunks, CHIPS)), dma((chunks, CHIPS)), dma((3,)), dma((tp - 1,)), dma((tp - 1,)),
        ],
        compiler_params=pltpu.CompilerParams(collective_id=0, has_side_effects=True, vmem_limit_bytes=VMEM_LIMIT),
        cost_estimate=pl.CostEstimate(flops=flops, bytes_accessed=2 * chunks * w_lm.size, transcendentals=tokens * w_lm.shape[-1]),
        name="layer_tail_and_head",
    )(attended, hidden, w_o, w_gate, w_up, w_down, w_lm.T, mlp_norm, final_norm, target)
    return log_norm, log_prob


def solution(mesh):
    tp = mesh.shape["tp"]

    def group_step(hidden, tree_mask, depth, ctx_len, block_table, score_id, k_cache, v_cache, attn_norm, w_q, w_k, w_v, w_o, mlp_norm, w_gate, w_up, w_down, final_norm, w_lm):
        requests, nodes, model = hidden.shape
        attended, k_out, v_out = attention(hidden, tree_mask, depth, ctx_len, block_table, k_cache, v_cache, attn_norm, w_q, w_k, w_v)
        log_norm, log_prob = tail(tp, attended, hidden.reshape(requests * nodes, model), w_o, w_gate, w_up, w_down, w_lm, mlp_norm, final_norm, score_id)
        return log_norm.reshape(requests, nodes), log_prob.reshape(requests, nodes), k_out, v_out

    request_spec = P("dp", None, None)
    node_spec = P("dp", None)
    cache_spec = P("dp", None, "tp", None)
    shared_spec = P(None)
    column_spec = P(None, "tp")
    row_spec = P("tp", None)
    in_specs = (request_spec, request_spec, node_spec, P("dp"), node_spec, node_spec, cache_spec, cache_spec, shared_spec, column_spec, column_spec, column_spec, row_spec, shared_spec, column_spec, column_spec, row_spec, shared_spec, column_spec)
    out_specs = (node_spec, node_spec, cache_spec, cache_spec)
    return jax.shard_map(group_step, mesh=mesh, in_specs=in_specs, out_specs=out_specs, check_vma=False)
```

time: 222 us -> 199 us (0.90)
  local copies, waits for them, and re-layouts: 18.8 us -> 4.12 us
  Pallas kernels: 200 us -> 190 us
    unnamed x28 -> x0, local copies, waits for them, and re-layouts: 13.1 us -> none
    pallas_call x1, Pallas kernels: 178 us -> 173 us  [tail(): pl.pallas_call(functools.partial(tail_body, tp), out_shape=[jax.ShapeDtyp...]
    pallas_call x1, Pallas kernels: 21.7 us -> 17.1 us  [attention(): pl.pallas_call(functools.partial(attention_body, per, pages), out_shape=[...]
where the time goes in v3:
time: 199 us; the launch traced here: 198 us
  Pallas kernels  190 us (95%)
  local copies, waits for them, and re-layouts  4.12 us (2%)
  other arithmetic  3.83 us (2%)
    pallas_call x1, Pallas kernels, tail(): pl.pallas_call(functools.partial(tail_body, tp), out_shape=[jax.ShapeDtyp...  173 us
    pallas_call x1, Pallas kernels, attention(): pl.pallas_call(functools.partial(attention_body, per, pages), out_shape=[...  17.1 us

profile of v3, /device:TPU:81, one launch (start us, length us, event | category | flops | bytes accessed | tf_op | source)
XLA Modules:
  0.0 198.3 jit_solution(11990861259128033927)
XLA Ops:
  0.6 0.8 add_convert_fusion
  1.4 0.1 mul.36
  1.5 3.0 %fusion = (f32[1024,128]{1,0:T(8,128)}, f32[1024,128]{1,0:T(8,128)}) fusion(f32[128]{0:T(128)S(1)} %get-tuple-element.20, f32[128]{0:T(128)S(1)} %get-tuple-element.21, f32[1024]{0:T(1024)S(1)} %mul.36), kind=kLoop, calls=%fused_computation.2 | loop fusion | flops 262144 | bytes 1053696 | tf_op jit(solution)/shard_map/mul | solution.py:120
  4.5 17.1 %tree_attention.1 = (bf16[1024,256]{1,0:T(8,128)(2,1)}, bf16[16,64,384]{2,1,0:T(8,128)(2,1)}, bf16[16,64,384]{2,1,0:T(8,128)(2,1)}) custom-call(s32[16]{0:T(128)} %ctx.1, s32[16,24]{1,0:T(8,128)} %table.1, bf16[1024,2048]{1,0:T(8,128)(2,1)} %bitcast.24, bf16[2048]{0:T(1024)(128)(2,1)} %gain.1, bf16[2048,256]{1,0:T(8,128)(2,1)} %w_q.1, ...), custom_call_target="tpu_custom_call" | custom-call | flops 1610612736 | bytes 4194304 | tf_op jit(solution)/shard_map/tree_attention/pallas_call | solution.py:126
  21.6 0.8 broadcast_in_dim.18
  22.4 0.6 broadcast_in_dim.19.target
  23.0 172.6 %layer_tail_and_head.1 = (f32[8,128]{1,0:T(8,128)}, f32[8,128]{1,0:T(8,128)}) custom-call(bf16[1024,256]{1,0:T(8,128)(2,1)} %get-tuple-element.9.att_hbm, bf16[1024,2048]{1,0:T(8,128)(2,1)} %bitcast.25, bf16[256,2048]{1,0:T(8,128)(2,1)} %wo_hbm.1, bf16[2048,1024]{1,0:T(8,128)(2,1)} %wg_hbm.1, bf16[2048,1024]{1,0:T(8,128)(2,1)} %wu_hbm.1, ...), custom_call_target="tpu_custom_call" | custom-call | flops 81201725440 | bytes 197001216 | tf_op jit(solution)/shard_map/layer_tail_and_head/pallas_call | solution.py:530
  195.6 1.3 reshape.66
  196.9 1.3 reshape.67
  (1 shorter events, 0.0 us)

commit v4 on v3

--- a/solution.py
+++ b/solution.py
@@ -452,10 +452,14 @@
     ag_forward(0, 0)
     rs_start(0, 1)
     wait_loads(2 * chunks + 1, len(loads))
-    for k in (1, 2, 3):
-        pair[chunks + k].wait_recv()
     ag_wait(0, 0)
-    mlp(0, lambda: rs_merge(0, 1))
+
+    def far_weights():
+        rs_merge(0, 1)
+        for k in (1, 2, 3):
+            pair[chunks + k].wait_recv()
+
+    mlp(0, far_weights)
     rs_start(1, 0)
     rs_merge(1, 0)
     mlp_end(0)
@@ -473,12 +477,13 @@
         mlp(p)
         rs_start(1, p)
 
-    def forward_and_end():
-        ag_forward(1, 1)
+    def two_ends():
+        mlp_end(1)
         attn_end(2)
 
     head(0, [(0, forward_and_start), (1, lambda: feed(1)), (2, lambda: rs_merge(0, 2)), (3, lambda: rs_merge(1, 1)),
-             (4, lambda: mlp_end(1)), (5, forward_and_end), (6, lambda: ag_wait(1, 1))])
+             (4, two_ends), (6, lambda: ag_forward(1, 1))])
+    ag_wait(1, 1)
     dd_wait(1)
     head(1, [(0, lambda: ag_forward(0, 2)), (1, lambda: feed(2)), (3, lambda: rs_merge(1, 2)), (4, lambda: mlp_end(2)),
              (6, lambda: ag_forward(1, 2))])

time: 199 us -> 199 us (level)
  no operation moved by 1% of the time
where the time goes in v4:
time: 199 us; the launch traced here: 198 us
  Pallas kernels  190 us (95%)
  local copies, waits for them, and re-layouts  4.12 us (2%)
  other arithmetic  3.83 us (2%)
    pallas_call x1, Pallas kernels, tail(): pl.pallas_call(functools.partial(tail_body, tp), out_shape=[jax.ShapeDtyp...  173 us
    pallas_call x1, Pallas kernels, attention(): pl.pallas_call(functools.partial(attention_body, per, pages), out_shape=[...  17.1 us

profile of v4, /device:TPU:81, one launch (start us, length us, event | category | flops | bytes accessed | tf_op | source)
XLA Modules:
  0.0 198.5 jit_solution(2672370057065714870)
XLA Ops:
  0.6 0.8 add_convert_fusion
  1.4 0.1 mul.36
  1.5 3.0 %fusion = (f32[1024,128]{1,0:T(8,128)}, f32[1024,128]{1,0:T(8,128)}) fusion(f32[128]{0:T(128)S(1)} %get-tuple-element.20, f32[128]{0:T(128)S(1)} %get-tuple-element.21, f32[1024]{0:T(1024)S(1)} %mul.36), kind=kLoop, calls=%fused_computation.2 | loop fusion | flops 262144 | bytes 1053696 | tf_op jit(solution)/shard_map/mul | solution.py:120
  4.5 17.1 %tree_attention.1 = (bf16[1024,256]{1,0:T(8,128)(2,1)}, bf16[16,64,384]{2,1,0:T(8,128)(2,1)}, bf16[16,64,384]{2,1,0:T(8,128)(2,1)}) custom-call(s32[16]{0:T(128)} %ctx.1, s32[16,24]{1,0:T(8,128)} %table.1, bf16[1024,2048]{1,0:T(8,128)(2,1)} %bitcast.24, bf16[2048]{0:T(1024)(128)(2,1)} %gain.1, bf16[2048,256]{1,0:T(8,128)(2,1)} %w_q.1, ...), custom_call_target="tpu_custom_call" | custom-call | flops 1610612736 | bytes 4194304 | tf_op jit(solution)/shard_map/tree_attention/pallas_call | solution.py:126
  21.6 0.8 broadcast_in_dim.18
  22.4 0.6 broadcast_in_dim.19.target
  23.0 172.8 %layer_tail_and_head.1 = (f32[8,128]{1,0:T(8,128)}, f32[8,128]{1,0:T(8,128)}) custom-call(bf16[1024,256]{1,0:T(8,128)(2,1)} %get-tuple-element.9.att_hbm, bf16[1024,2048]{1,0:T(8,128)(2,1)} %bitcast.25, bf16[256,2048]{1,0:T(8,128)(2,1)} %wo_hbm.1, bf16[2048,1024]{1,0:T(8,128)(2,1)} %wg_hbm.1, bf16[2048,1024]{1,0:T(8,128)(2,1)} %wu_hbm.1, ...), custom_call_target="tpu_custom_call" | custom-call | flops 81201725440 | bytes 197001216 | tf_op jit(solution)/shard_map/layer_tail_and_head/pallas_call | solution.py:535
  195.8 1.3 reshape.66
  197.1 1.3 reshape.67
  (1 shorter events, 0.0 us)
